TPU v7x, 32 devices: a whole 2x2x4 slice. The times are simulated.
32 devices in a mesh: fsdp: 2 (over y), trow: 4 (over x, core), tcol: 4 (over z).
Axes of the slice: x: 2, y: 2, z: 4, core: 2. Of those that a mesh axis runs over, the one named last changes fastest.
Arguments:
- tokens: bfloat16 [512, 4096], P('fsdp', 'tcol'), may hold values from -100 to 100
- w_up: bfloat16 [4096, 16384], P('tcol', ('fsdp', 'trow')), may hold values from -0.1875 to 0.1875
- w_down: bfloat16 [16384, 4096], P(('fsdp', 'trow'), 'tcol'), may hold values from -0.046875 to 0.046875
- cotangent: bfloat16 [512, 4096], P('fsdp', 'tcol'), may hold values from -6 to 6
Outputs:
- mixed: bfloat16 [512, 4096], P('fsdp', 'tcol')
- input_gradient: bfloat16 [512, 4096], P('fsdp', 'tcol')
- grad_up: bfloat16 [4096, 16384], P('tcol', ('fsdp', 'trow'))
- grad_down: bfloat16 [16384, 4096], P(('fsdp', 'trow'), 'tcol')
All inputs are finite; a program needn't handle non-finite values.
Results may differ from a plain program's by a relative error of at most 0.02.
Values may be sent and summed in bfloat16 or wider, within the bound.
A program may use at most 128 MiB of HBM per device.

v0:
```python
import jax
import jax.numpy as jnp
from jax import lax
from jax.sharding import PartitionSpec as P


def gelu_value(pre):
    phi = 0.5 * (1.0 + jax.scipy.special.erf(pre * 0.7071067811865476))
    return pre * phi


def gelu_slope(pre):
    phi = 0.5 * (1.0 + jax.scipy.special.erf(pre * 0.7071067811865476))
    return phi + pre * jnp.exp(-0.5 * pre * pre) * 0.3989422804014327


def contract(left, right, left_dim, right_dim):
    return lax.dot_general(
        left, right, (((left_dim,), (right_dim,)), ((), ())), preferred_element_type=jnp.float32
    )


def local(tokens, w_up, w_down, cotangent):
    width = tokens.shape[1] * lax.axis_size("tcol")
    input_float = tokens.astype(jnp.float32)
    cot_all = lax.all_gather(cotangent, "fsdp", axis=0, tiled=True)
    sum_one, sum_two = lax.psum(
        (jnp.sum(input_float, axis=1), jnp.sum(input_float * input_float, axis=1)), "tcol"
    )
    token_mean = sum_one / width
    var = sum_two / width - token_mean * token_mean
    inverse_stddev = lax.rsqrt(var + 1e-05)
    centered_scaled = (input_float - token_mean[:, None]) * inverse_stddev[:, None]
    normalized_rows = centered_scaled.astype(jnp.bfloat16)
    normed_all = lax.all_gather(normalized_rows, "fsdp", axis=0, tiled=True)
    dhid_part = contract(cot_all, w_down, 1, 1).astype(jnp.bfloat16)
    dhid = lax.psum_scatter(dhid_part, "tcol", scatter_dimension=0, tiled=True).astype(jnp.float32)
    pre_part = contract(normed_all, w_up, 1, 0).astype(jnp.bfloat16)
    pre = lax.psum_scatter(pre_part, "tcol", scatter_dimension=0, tiled=True).astype(jnp.float32)
    hidden = lax.all_gather(gelu_value(pre).astype(jnp.bfloat16), "tcol", axis=0, tiled=True)
    dpre = lax.all_gather(
        (dhid * gelu_slope(pre)).astype(jnp.bfloat16), "tcol", axis=0, tiled=True
    )
    branch_part = contract(hidden, w_down, 1, 0).astype(jnp.bfloat16)
    branch = lax.psum_scatter(branch_part, "fsdp", scatter_dimension=0, tiled=True)
    branch = lax.psum(branch, "trow").astype(jnp.float32)
    mixed = (input_float + branch).astype(jnp.bfloat16)
    grad_down = contract(hidden, cot_all, 0, 0).astype(jnp.bfloat16)
    dnorm_part = contract(dpre, w_up, 1, 1).astype(jnp.bfloat16)
    dnorm = lax.psum_scatter(dnorm_part, "fsdp", scatter_dimension=0, tiled=True)
    normed_gradient = lax.psum(dnorm, "trow").astype(jnp.float32)
    grad_up = contract(normed_all, dpre, 0, 0).astype(jnp.bfloat16)
    mean_first, mean_second = lax.psum(
        (jnp.sum(normed_gradient, axis=1), jnp.sum(normed_gradient * centered_scaled, axis=1)),
        "tcol",
    )
    first_moment = mean_first / width
    second_moment = mean_second / width
    input_gradient = cotangent.astype(jnp.float32) + inverse_stddev[:, None] * (
        normed_gradient - first_moment[:, None] - centered_scaled * second_moment[:, None]
    )
    return (mixed, input_gradient.astype(jnp.bfloat16), grad_up, grad_down)


def solution(mesh):
    return jax.shard_map(
        local,
        mesh=mesh,
        in_specs=(
            P("fsdp", "tcol"),
            P("tcol", ("fsdp", "trow")),
            P(("fsdp", "trow"), "tcol"),
            P("fsdp", "tcol"),
        ),
        out_specs=(
            P("fsdp", "tcol"),
            P("fsdp", "tcol"),
            P("tcol", ("fsdp", "trow")),
            P(("fsdp", "trow"), "tcol"),
        ),
        check_vma=False,
    )
```

profile of v0, /device:TPU:0, one launch (start us, length us, event | category | flops | bytes accessed | tf_op | source)
XLA Modules:
  0.0 359.4 jit_solution(15157938787356180238)
XLA Ops:
  7.2 0.0 all-gather.5.cloned.1.call-start
  7.2 1.3 convert_reduce_fusion
  8.5 13.5 %all-reduce.1 = (f32[256]{0:T(256)S(1)}, f32[256]{0:T(256)S(1)}) all-reduce(f32[256]{0:T(256)S(1)} %get-tuple-element.7, f32[256]{0:T(256)S(1)} %get-tuple-element.6), channel_id=1, replica_groups=mesh['fsdp'=2,'trow'=4,'tcol'=4] {'tcol'}, use_global_device_ids=true, to_apply=%region_3.0 | all-reduce | flops 512 | bytes 4096 | tf_op jit(solution)/shard_map/psum | solution.py:27
  22.0 2.1 fusion.7
  24.1 0.0 all-gather.5.cloned.1.call-update
  24.1 0.0 all-gather.9.cloned.1.call-start
  24.2 0.7 all-gather.9.cloned.1.call-update
  24.9 0.0 reduce-scatter.5.cloned.1.call-start
  24.9 18.9 %all-gather.5.cloned.1.call-done = bf16[512,1024]{1,0:T(8,128)(2,1)} async-done(((bf16[256,1024]{1,0:T(8,128)(2,1)}), bf16[512,1024]{1,0:T(8,128)(2,1)}) %all-gather.5.cloned.1.call-update) | async-done | bytes 1048592 | tf_op jit(solution)/shard_map/all_gather | solution.py:35
  43.8 6.2 %convolution_convert_fusion.3 = bf16[512,2048]{1,0:T(8,128)(2,1)} fusion(bf16[512,1024]{1,0:T(8,128)(2,1)} %all-gather.5.cloned.1.call-done, bf16[1024,2048]{1,0:T(8,128)(2,1)} %param.5), kind=kOutput, calls=%fused_computation.3 | convolution fusion | flops 2148532224 | bytes 7340032 | tf_op jit(solution)/shard_map/dot_general | solution.py:18
  49.9 0.0 reduce-scatter.5.cloned.1.call-update
  49.9 0.0 reduce-scatter.9.cloned.1.call-start
  50.0 16.6 %all-gather.9.cloned.1.call-done = bf16[512,1024]{1,0:T(8,128)(2,1)} async-done(((bf16[256,1024]{1,0:T(8,128)(2,1)}), bf16[512,1024]{1,0:T(8,128)(2,1)}) %all-gather.9.cloned.1.call-update) | async-done | bytes 1048592 | tf_op jit(solution)/shard_map/all_gather | solution.py:26
  66.6 6.2 %convolution_convert_fusion.2 = bf16[512,2048]{1,0:T(8,128)(2,1)} fusion(bf16[512,1024]{1,0:T(8,128)(2,1)} %all-gather.9.cloned.1.call-done, bf16[2048,1024]{1,0:T(8,128)(2,1)} %param.6), kind=kOutput, calls=%fused_computation.2 | convolution fusion | flops 2148532224 | bytes 7340032 | tf_op jit(solution)/shard_map/dot_general | solution.py:18
  72.8 0.0 reduce-scatter.9.cloned.1.call-update
  72.8 0.0 all-gather.7.cloned.1.call-start
  72.9 40.3 %reduce-scatter.5.cloned.1.call-done = bf16[128,2048]{1,0:T(8,128)(2,1)} async-done(((bf16[512,2048]{1,0:T(8,128)(2,1)}), bf16[128,2048]{1,0:T(8,128)(2,1)}) %reduce-scatter.5.cloned.1.call-update) | async-done | bytes 524304 | tf_op jit(solution)/shard_map/reduce_scatter | solution.py:39
  113.2 45.6 %reduce-scatter.9.cloned.1.call-done = bf16[128,2048]{1,0:T(8,128)(2,1)} async-done(((bf16[512,2048]{1,0:T(8,128)(2,1)}), bf16[128,2048]{1,0:T(8,128)(2,1)}) %reduce-scatter.9.cloned.1.call-update) | async-done | bytes 524304 | tf_op jit(solution)/shard_map/reduce_scatter | solution.py:37
  158.7 2.7 fusion.18
  161.4 0.0 all-gather.7.cloned.1.call-update
  161.5 0.0 all-gather.11.cloned.1.call-start
  161.5 0.5 all-gather.11.cloned.1.call-update
  162.0 0.0 reduce-scatter.7.cloned.1.call-start
  162.1 44.4 %all-gather.7.cloned.1.call-done = bf16[512,2048]{1,0:T(8,128)(2,1)} async-done(((bf16[128,2048]{1,0:T(8,128)(2,1)}), bf16[512,2048]{1,0:T(8,128)(2,1)}) %all-gather.7.cloned.1.call-update) | async-done | bytes 2097168 | tf_op jit(solution)/shard_map/all_gather | solution.py:40
  206.5 6.1 %convolution_convert_fusion.5 = bf16[512,1024]{1,0:T(8,128)(2,1)} fusion(bf16[512,2048]{1,0:T(8,128)(2,1)} %all-gather.7.cloned.1.call-done, bf16[2048,1024]{1,0:T(8,128)(2,1)} %param.6), kind=kOutput, calls=%fused_computation.17 | convolution fusion | flops 2148007936 | bytes 7340032 | tf_op jit(solution)/shard_map/dot_general | solution.py:18
  212.6 0.0 reduce-scatter.7.cloned.1.call-update
  212.6 0.0 copy-start.2
  212.6 0.0 copy-start.5
  212.6 0.0 reduce-scatter.11.cloned.1.call-start
  212.7 40.3 %all-gather.11.cloned.1.call-done = bf16[512,2048]{1,0:T(8,128)(2,1)} async-done(((bf16[128,2048]{1,0:T(8,128)(2,1)}), bf16[512,2048]{1,0:T(8,128)(2,1)}) %all-gather.11.cloned.1.call-update) | async-done | bytes 2097168 | tf_op jit(solution)/shard_map/all_gather | solution.py:41
  253.0 6.2 %convolution_convert_fusion.4 = bf16[512,1024]{1,0:T(8,128)(2,1)} fusion(bf16[512,2048]{1,0:T(8,128)(2,1)} %all-gather.11.cloned.1.call-done, bf16[1024,2048]{1,0:T(8,128)(2,1)} %param.5), kind=kOutput, calls=%fused_computation.16 | convolution fusion | flops 2148007936 | bytes 7340032 | tf_op jit(solution)/shard_map/dot_general | solution.py:18
  259.1 0.0 reduce-scatter.11.cloned.1.call-update
  259.1 0.2 all-reduce.5.cloned.1.call-start
  259.4 15.6 %reduce-scatter.7.cloned.1.call-done = bf16[256,1024]{1,0:T(8,128)(2,1)} async-done(((bf16[512,1024]{1,0:T(8,128)(2,1)}), bf16[256,1024]{1,0:T(8,128)(2,1)}) %reduce-scatter.7.cloned.1.call-update) | async-done | bytes 524304 | tf_op jit(solution)/shard_map/reduce_scatter | solution.py:45
  275.0 23.2 %reduce-scatter.11.cloned.1.call-done = bf16[256,1024]{1,0:T(8,128)(2,1)} async-done(((bf16[512,1024]{1,0:T(8,128)(2,1)}), bf16[256,1024]{1,0:T(8,128)(2,1)}) %reduce-scatter.11.cloned.1.call-update) | async-done | bytes 524304 | tf_op jit(solution)/shard_map/reduce_scatter | solution.py:50
  298.2 0.0 all-reduce.5.cloned.1.call-update
  298.3 0.0 copy-done.2
  298.3 0.0 copy-done.5
  298.3 0.0 copy-start.3
  298.3 0.0 copy-start.4
  298.3 4.4 %convolution_convert_fusion = bf16[2048,1024]{1,0:T(8,128)(2,1)} fusion(bf16[512,2048]{1,0:T(8,128)(2,1)S(1)} %copy-done.2, bf16[512,1024]{1,0:T(8,128)(2,1)S(1)} %copy-done.5), kind=kOutput, calls=%fused_computation | convolution fusion | flops 2149580800 | bytes 7340032 | tf_op jit(solution)/shard_map/dot_general | solution.py:18
  302.7 0.0 copy-done.3
  302.7 0.0 copy-done.4
  302.7 0.0 copy-start
  302.7 0.0 copy-start.1
  302.7 4.4 %convolution_convert_fusion.1 = bf16[1024,2048]{1,0:T(8,128)(2,1)} fusion(bf16[512,1024]{1,0:T(8,128)(2,1)S(1)} %copy-done.4, bf16[512,2048]{1,0:T(8,128)(2,1)S(1)} %copy-done.3), kind=kOutput, calls=%fused_computation.1 | convolution fusion | flops 2149580800 | bytes 7340032 | tf_op jit(solution)/shard_map/dot_general | solution.py:18
  307.2 29.9 %all-reduce.5.cloned.1.call-done = (bf16[256,1024]{1,0:T(8,128)(2,1)}, bf16[256,1024]{1,0:T(8,128)(2,1)}) async-done(((bf16[256,1024]{1,0:T(8,128)(2,1)}, bf16[256,1024]{1,0:T(8,128)(2,1)}), (bf16[256,1024]{1,0:T(8,128)(2,1)}, bf16[256,1024]{1,0:T(8,128)(2,1)})) %all-reduce.5.cloned.1.call-update) | async-done | bytes 1048592 | tf_op jit(solution)/shard_map/psum | solution.py:46
  337.1 0.0 copy-done
  337.1 1.5 convert_reduce_fusion.1
  338.5 11.7 %all-reduce = (f32[256]{0:T(256)S(1)}, f32[256]{0:T(256)S(1)}) all-reduce(f32[256]{0:T(256)S(1)} %get-tuple-element.5, f32[256]{0:T(256)S(1)} %get-tuple-element.4), channel_id=1, replica_groups=mesh['fsdp'=2,'trow'=4,'tcol'=4] {'tcol'}, use_global_device_ids=true, to_apply=%region_13.0 | all-reduce | flops 512 | bytes 4096 | tf_op jit(solution)/shard_map/psum | solution.py:53
  350.2 0.0 copy-done.1
  350.2 2.6 fusion.3
  (2 shorter events, 0.0 us)
Async XLA Ops:
  7.2 36.6 %all-gather.5.cloned.1.call-start = ((), (), s32[]{:S(2)}) async-start(), calls=%async_computation.4 | async-start | bytes 1572864 | tf_op jit(solution)/shard_map/all_gather | solution.py:35
  24.1 42.5 %all-gather.9.cloned.1.call-start = ((), (), s32[]{:S(2)}) async-start(), calls=%async_computation.8 | async-start | bytes 1572864 | tf_op jit(solution)/shard_map/all_gather | solution.py:26
  24.9 88.3 %reduce-scatter.5.cloned.1.call-start = ((), (), s32[]{:S(2)}) async-start(), calls=%async_computation.5 | async-start | bytes 2621440 | tf_op jit(solution)/shard_map/reduce_scatter | solution.py:39
  49.9 108.8 %reduce-scatter.9.cloned.1.call-start = ((), (), s32[]{:S(2)}) async-start(), calls=%async_computation.9 | async-start | bytes 2621440 | tf_op jit(solution)/shard_map/reduce_scatter | solution.py:37
  72.8 133.6 %all-gather.7.cloned.1.call-start = ((), (), s32[]{:S(2)}) async-start(), calls=%async_computation.6 | async-start | bytes 2621440 | tf_op jit(solution)/shard_map/all_gather | solution.py:40
  161.5 91.5 %all-gather.11.cloned.1.call-start = ((), (), s32[]{:S(2)}) async-start(), calls=%async_computation.10 | async-start | bytes 2621440 | tf_op jit(solution)/shard_map/all_gather | solution.py:41
  162.0 113.0 %reduce-scatter.7.cloned.1.call-start = ((), (), s32[]{:S(2)}) async-start(), calls=%async_computation.7 | async-start | bytes 1572864 | tf_op jit(solution)/shard_map/reduce_scatter | solution.py:45
  212.6 85.6 %copy-start.2 = (bf16[512,2048]{1,0:T(8,128)(2,1)S(1)}, bf16[512,2048]{1,0:T(8,128)(2,1)}, u32[]{:S(2)}) copy-start(bf16[512,2048]{1,0:T(8,128)(2,1)} %all-gather.7.cloned.1.call-done) | copy-start | bytes 6291460
  212.6 85.6 %copy-start.5 = (bf16[512,1024]{1,0:T(8,128)(2,1)S(1)}, bf16[512,1024]{1,0:T(8,128)(2,1)}, u32[]{:S(2)}) copy-start(bf16[512,1024]{1,0:T(8,128)(2,1)} %all-gather.9.cloned.1.call-done) | copy-start | bytes 3145732
  212.6 85.6 %reduce-scatter.11.cloned.1.call-start = ((), (), s32[]{:S(2)}) async-start(), calls=%async_computation.11 | async-start | bytes 1572864 | tf_op jit(solution)/shard_map/reduce_scatter | solution.py:50
  259.1 77.9 %all-reduce.5.cloned.1.call-start = ((), (), s32[]{:S(2)}) async-start(), calls=%async_computation.12 | async-start | bytes 2097152 | tf_op jit(solution)/shard_map/psum | solution.py:46
  298.3 4.4 %copy-start.3 = (bf16[512,2048]{1,0:T(8,128)(2,1)S(1)}, bf16[512,2048]{1,0:T(8,128)(2,1)}, u32[]{:S(2)}) copy-start(bf16[512,2048]{1,0:T(8,128)(2,1)} %all-gather.11.cloned.1.call-done) | copy-start | bytes 6291460
  298.3 4.4 %copy-start.4 = (bf16[512,1024]{1,0:T(8,128)(2,1)S(1)}, bf16[512,1024]{1,0:T(8,128)(2,1)}, u32[]{:S(2)}) copy-start(bf16[512,1024]{1,0:T(8,128)(2,1)} %all-gather.5.cloned.1.call-done) | copy-start | bytes 3145732
  302.7 34.3 %copy-start = (bf16[256,1024]{1,0:T(8,128)(2,1)S(1)}, bf16[256,1024]{1,0:T(8,128)(2,1)}, u32[]{:S(2)}) copy-start(bf16[256,1024]{1,0:T(8,128)(2,1)} %param.4) | copy-start | bytes 1572868
  302.7 47.5 %copy-start.1 = (bf16[256,1024]{1,0:T(8,128)(2,1)S(1)}, bf16[256,1024]{1,0:T(8,128)(2,1)}, u32[]{:S(2)}) copy-start(bf16[256,1024]{1,0:T(8,128)(2,1)} %param.7) | copy-start | bytes 1572868
Sparse Core Ops, SparseCore 0:
  24.2 19.4 all-gather.4
  45.3 21.2 all-gather.8
  69.5 43.6 reduce-scatter.4
  115.9 42.8 reduce-scatter.8
  161.6 44.8 all-gather.6
  208.5 44.4 all-gather.10
  255.8 19.1 reduce-scatter.6
  277.8 20.3 reduce-scatter.10
  300.7 36.3 all-reduce.4
where the time goes:
time: 360 us; the launch traced here: 359 us
  waiting for transfers between devices  276 us (77%)
  matrix products  33.5 us (9%)
  blocking collectives  25.2 us (7%)
  between operations  13.9 us (4%)
  other arithmetic  10.2 us (3%)
    reduce_scatter x1, waiting for transfers between devices, local(): lax.psum_scatter(dhid_part, 'tcol', scatter_dimension=0, tiled=True)  45.6 us
    all_gather x1, waiting for transfers between devices, local(): lax.all_gather(gelu_value(pre).astype(jnp.bfloat16), 'tcol', axis=0, tile...  44.4 us
    all_gather x1, waiting for transfers between devices, local(): lax.all_gather((dhid * gelu_slope(pre)).astype(jnp.bfloat16), 'tcol', axi...  40.3 us
    reduce_scatter x1, waiting for transfers between devices, local(): lax.psum_scatter(pre_part, 'tcol', scatter_dimension=0, tiled=True)  40.3 us
    dot_general x6, matrix products, contract(): lax.dot_general(left, right, (((left_dim,), (right_dim,)), ((), ())), pre...  33.5 us
    psum x1, waiting for transfers between devices, local(): branch = lax.psum(branch, 'trow').astype(jnp.float32)  29.9 us
    reduce_scatter x1, waiting for transfers between devices, local(): lax.psum_scatter(dnorm_part, 'fsdp', scatter_dimension=0, tiled=True)  23.2 us
    all_gather x1, waiting for transfers between devices, local(): normed_all = lax.all_gather(normalized_rows, 'fsdp', axis=0, tiled=True)  18.9 us
  transfers between devices with their start and end apart: 9, of which 9 were waited for; matrix products, arithmetic and copies ran while one was open for 9% of the time, Pallas kernels for 0%

commit v1 on v0

v1 whole, which is shorter than its diff:
```python
import functools

import jax
import jax.numpy as jnp
from jax import lax
from jax.experimental import pallas as pl
from jax.experimental.pallas import tpu as pltpu
from jax.sharding import PartitionSpec as P

MESH = pl.DeviceIdType.MESH
BF16 = jnp.bfloat16
F32 = jnp.float32
SQRT_HALF = 0.7071067811865476
INV_SQRT_2PI = 0.3989422804014327
EPS = 1e-05
END_LAG = 9
MID_LAG = 2


def gelu_value(pre):
    phi = 0.5 * (1.0 + jax.scipy.special.erf(pre * SQRT_HALF))
    return pre * phi


def gelu_slope(pre):
    phi = 0.5 * (1.0 + jax.scipy.special.erf(pre * SQRT_HALF))
    return phi + pre * jnp.exp(-0.5 * pre * pre) * INV_SQRT_2PI


def contract(left, right, left_dim, right_dim):
    return lax.dot_general(
        left, right, (((left_dim,), (right_dim,)), ((), ())), preferred_element_type=F32
    )


def line_kernel(
    sizes,
    tok_in, up_in, down_in, cot_in,
    mixed_out, grad_out, hid_out, dpre_out, norm_out, cot_out,
    xall, call, nall, wu, wd, tx, rx, rm, hd,
    st_tx, st_rx, flip, ms, acc, rs_tx, rs_rx, keep, y_tx, y_rx, ag_rx, mix_v, st2, f_tx, f_rx, ig_v,
    load_sem, wu_sem, wd_sem, tx_sem, rx_sem, rm_sem, hs_sem, hr_sem, ho_sem,
    ss_sem, sr_sem, ys_sem, yr_sem, rss_sem, rsr_sem, yqs_sem, yqr_sem, ags_sem, agr_sem,
    fs_sem, fr_sem, out_sem,
):
    nz, nt, rows, depth, ff, tb_size, fb_size = sizes
    nfb = ff // fb_size
    ntb = 2 * rows // tb_size
    half = ntb // 2
    nb = ntb * nfb
    quarter = depth // nt
    width = depth * nz
    y = lax.axis_index("fsdp")
    tr = lax.axis_index("trow")
    j = lax.axis_index("tcol")
    mid_low = nz // 2 - 1
    is_mid = jnp.logical_or(j == mid_low, j == mid_low + 1)
    is_end = jnp.logical_not(is_mid)
    inner = jnp.where(j <= mid_low, j + 1, j - 1)
    outer = jnp.where(j <= mid_low, jnp.maximum(j - 1, 0), jnp.minimum(j + 1, nz - 1))
    lag = jnp.where(is_mid, MID_LAG, END_LAG)

    def at(yy, tt, jj):
        return {"fsdp": yy, "trow": tt, "tcol": jj}

    def remote(src, dst, send, recv, device):
        return pltpu.make_async_remote_copy(
            src_ref=src, dst_ref=dst, send_sem=send, recv_sem=recv,
            device_id=device, device_id_type=MESH,
        )

    def z_peer(d):
        return lax.rem(j + d, nz)

    def t_peer(d):
        return lax.rem(tr + d, nt)

    here = at(y, tr, j)
    other = 1 - y

    own = pl.ds(0, rows)
    far = pl.ds(rows, rows)
    tok_load = pltpu.make_async_copy(tok_in, xall.at[own], load_sem.at[0])
    cot_load = pltpu.make_async_copy(cot_in, call.at[own], load_sem.at[1])

    def wd_load(f):
        return pltpu.make_async_copy(
            down_in.at[pl.ds(pl.multiple_of(f * fb_size, fb_size), fb_size)], wd.at[f], wd_sem.at[f]
        )

    def wu_load(f):
        return pltpu.make_async_copy(
            up_in.at[:, pl.ds(pl.multiple_of(f * fb_size, fb_size), fb_size)], wu.at[f], wu_sem.at[f]
        )

    tok_load.start()
    cot_load.start()
    for f in range(nfb):
        wd_load(f).start()
        wu_load(f).start()

    barrier = pltpu.get_barrier_semaphore()
    partners = [at(y, tr, z_peer(d)) for d in range(1, nz)]
    partners += [at(other, tr, z_peer(d)) for d in range(nz)]
    partners += [at(y, t_peer(d), j) for d in range(1, nt)]
    for device in partners:
        pl.semaphore_signal(barrier, inc=1, device_id=device, device_id_type=MESH)
    pl.semaphore_wait(barrier, len(partners))

    lane = lax.broadcasted_iota(jnp.int32, (tb_size, 128), 1)

    def pair_tile(one, two):
        return jnp.where(lane == 0, one, jnp.where(lane == 1, two, 0.0))

    tok_load.wait()

    def stat_step(i, carry):
        at_rows = pl.ds(pl.multiple_of(i * tb_size, tb_size), tb_size)
        x = xall[at_rows, :].astype(F32)
        st2[at_rows, :] = pair_tile(
            jnp.sum(x, axis=1, keepdims=True), jnp.sum(x * x, axis=1, keepdims=True)
        )
        return carry

    lax.fori_loop(0, half, stat_step, 0)
    stats = st2[...].T[0:8]
    st_tx[...] = stats
    st_rx[0, j] = stats

    def stat_copy(k, rel, d):
        target = at(y if rel == 0 else other, tr, z_peer(d))
        return remote(st_tx, st_rx.at[rel, j], ss_sem.at[k], sr_sem.at[rel, d], target)

    stat_list = [(0, d) for d in range(1, nz)] + [(1, d) for d in range(nz)]
    for k, (rel, d) in enumerate(stat_list):
        stat_copy(k, rel, d).start()
    cot_load.wait()
    y_cot = remote(call.at[own], call.at[far], ys_sem.at[0], yr_sem.at[0], at(other, tr, j))
    y_tok = remote(xall.at[own], xall.at[far], ys_sem.at[1], yr_sem.at[1], at(other, tr, j))
    y_cot.start()
    y_tok.start()

    def normalize(rel):
        for d in range(1 if rel == 0 else 0, nz):
            source = lax.rem(j + nz - d, nz)
            remote(st_tx, st_rx.at[rel, source], ss_sem.at[0], sr_sem.at[rel, d], here).wait_recv()
        total = st_rx[rel, 0]
        for z in range(1, nz):
            total = total + st_rx[rel, z]
        total = total / width
        mean = total[0:1]
        rstd = lax.rsqrt(total[1:2] - mean * mean + EPS)
        flip[...] = jnp.zeros_like(flip)
        flip[0:1] = mean
        flip[1:2] = rstd
        back = flip[...].T
        ms[rel] = back

        def step(i, carry):
            in_rows = pl.ds(pl.multiple_of(i * tb_size, tb_size), tb_size)
            at_rows = pl.ds(pl.multiple_of(rel * rows + i * tb_size, tb_size), tb_size)
            x = xall[at_rows, :].astype(F32)
            tile = ms[rel, in_rows, :]
            nall[at_rows, :] = ((x - tile[:, 0:1]) * tile[:, 1:2]).astype(BF16)
            return carry

        lax.fori_loop(0, half, step, 0)
        span = own if rel == 0 else far
        pltpu.make_async_copy(nall.at[span], norm_out.at[span], out_sem.at[rel]).start()
        pltpu.make_async_copy(call.at[span], cot_out.at[span], out_sem.at[2 + rel]).start()

    def inward(k, s):
        return (
            remote(tx.at[k, s], rx.at[k, s], tx_sem.at[k, s], rx_sem.at[k, s], at(y, tr, inner)),
            remote(tx.at[k, s], rm.at[k, s], tx_sem.at[k, s], rm_sem.at[k, s], at(y, tr, inner)),
        )

    def outward(k, s):
        return remote(hd.at[k, s], hd.at[k, s], hs_sem.at[k, s], hr_sem.at[k, s], at(y, tr, outer))

    def send_partial(k, s, part):
        to_mid, across = inward(k, s)

        @pl.when(is_end)
        def _():
            tx[k, s] = part.astype(BF16)
            to_mid.start()

        @pl.when(is_mid)
        def _():
            to_mid.wait_recv()
            tx[k, s] = (part + rx[k, s].astype(F32)).astype(BF16)
            across.start()

    def block_rows(t):
        return pl.ds(pl.multiple_of(t * tb_size, tb_size), tb_size)

    def partial_stage(s):
        t = s // nfb
        f = lax.rem(s, nfb)

        @pl.when(s < nfb)
        def _():
            wd_load(f).wait()
            wu_load(f).wait()

        @pl.when(s == nb // 2)
        def _():
            y_cot.wait_recv()
            y_tok.wait_recv()
            normalize(1)

        send_partial(0, s, contract(call[block_rows(t), :], wd[f], 1, 1))

        @pl.when(s == 0)
        def _():
            normalize(0)

        send_partial(1, s, contract(nall[block_rows(t), :], wu[f], 1, 0))

    def act_stage(e):
        for k in range(2):
            inward(k, e)[1].wait_recv()

        def step(i, carry):
            r = pl.ds(pl.multiple_of(i * 16, 16), 16)
            dhid = tx[0, e, r, :].astype(F32) + rm[0, e, r, :].astype(F32)
            pre = tx[1, e, r, :].astype(F32) + rm[1, e, r, :].astype(F32)
            phi = 0.5 * (1.0 + lax.erf(pre * SQRT_HALF))
            slope = phi + pre * jnp.exp(-0.5 * pre * pre) * INV_SQRT_2PI
            hd[0, e, r, :] = (pre * phi).astype(BF16)
            hd[1, e, r, :] = (dhid * slope).astype(BF16)
            return carry

        lax.fori_loop(0, tb_size // 16, step, 0)
        for k in range(2):
            outward(k, e).start()

    def hbm_copy(k, e):
        out = hid_out if k == 0 else dpre_out
        cols = pl.ds(pl.multiple_of(lax.rem(e, nfb) * fb_size, fb_size), fb_size)
        return pltpu.make_async_copy(hd.at[k, e], out.at[block_rows(e // nfb), cols], ho_sem.at[k, e])

    def rs_copy(t, d):
        return remote(
            rs_tx.at[t, d - 1], rs_rx.at[t, d - 1], rss_sem.at[t, d - 1], rsr_sem.at[t, d - 1],
            at(y, t_peer(d), j),
        )

    def columns(q):
        return pl.ds(pl.multiple_of(q * quarter, quarter), quarter)

    def use_stage(e):
        @pl.when(is_end)
        def _():
            for k in range(2):
                outward(k, e).wait_recv()

        for k in range(2):
            hbm_copy(k, e).start()
        f = lax.rem(e, nfb)
        t = e // nfb

        @pl.when(f == 0)
        def _():
            acc[...] = jnp.zeros_like(acc)

        acc[0] += contract(hd[0, e], wd[f], 1, 0)
        acc[1] += contract(hd[1, e], wu[f], 1, 1)

        @pl.when(f == nfb - 1)
        def _():
            for d in range(1, nt):
                for k in range(2):
                    rs_tx[t, d - 1, k] = acc[k, :, columns(t_peer(d))].astype(BF16)
                rs_copy(t, d).start()
            for k in range(2):
                keep[t, k] = acc[k, :, columns(tr)]

    def yq_copy(t):
        return remote(y_tx.at[t], y_rx.at[t], yqs_sem.at[t], yqr_sem.at[t], at(other, tr, j))

    def ag_copy(t, d):
        return remote(
            ag_rx.at[t, tr], ag_rx.at[t, tr], ags_sem.at[t, d - 1], agr_sem.at[t, d - 1],
            at(y, t_peer(d), j),
        )

    def row_sum_stage(t):
        for d in range(1, nt):
            rs_copy(t, d).wait_recv()
        for k in range(2):
            total = keep[t, k]
            for d in range(1, nt):
                total = total + rs_rx[t, d - 1, k].astype(F32)
            keep[t, k] = total

        @pl.when(t >= half)
        def _():
            for k in range(2):
                y_tx[t - half, k] = keep[t, k].astype(BF16)
            yq_copy(t - half).start()

    def gather_stage(t):
        yq_copy(t).wait_recv()
        for k in range(2):
            ag_rx[t, tr, k] = (keep[t, k] + y_rx[t, k].astype(F32)).astype(BF16)
        for d in range(1, nt):
            ag_copy(t, d).start()

    def xhat_of(t, q):
        tile = ms[0, block_rows(t), :]
        x = xall[block_rows(t), q * quarter:(q + 1) * quarter].astype(F32)
        return x, (x - tile[:, 0:1]) * tile[:, 1:2]

    def finish_stage(t):
        for d in range(1, nt):
            source = lax.rem(tr + nt - d, nt)
            remote(
                ag_rx.at[t, source], ag_rx.at[t, source], ags_sem.at[t, d - 1],
                agr_sem.at[t, d - 1], here,
            ).wait_recv()
        one = jnp.zeros((tb_size, 1), F32)
        two = jnp.zeros((tb_size, 1), F32)
        for q in range(nt):
            x, xhat = xhat_of(t, q)
            mix_v[block_rows(t), q * quarter:(q + 1) * quarter] = (
                x + ag_rx[t, q, 0].astype(F32)
            ).astype(BF16)
            dn = ag_rx[t, q, 1].astype(F32)
            one += jnp.sum(dn, axis=1, keepdims=True)
            two += jnp.sum(dn * xhat, axis=1, keepdims=True)
        st2[block_rows(t), :] = pair_tile(one, two)

    def step(s, carry):
        @pl.when(s < nb)
        def _():
            partial_stage(s)

        e = s - lag
        valid = jnp.logical_and(e >= 0, e < nb)

        @pl.when(jnp.logical_and(valid, is_mid))
        def _():
            act_stage(e)

        @pl.when(valid)
        def _():
            use_stage(e)

        def done_block(shift, low, high, stage):
            k = e - shift - (nfb - 1)
            t = k // nfb
            ok = jnp.logical_and(k >= low * nfb, k < high * nfb)

            @pl.when(jnp.logical_and(ok, lax.rem(k, nfb) == 0))
            def _():
                stage(t - low if low else t)

        done_block(2, 0, ntb, row_sum_stage)
        done_block(4, half, ntb, gather_stage)
        done_block(6, half, ntb, finish_stage)
        return carry

    lax.fori_loop(0, nb + max(END_LAG, MID_LAG) + 6, step, 0)

    pltpu.make_async_copy(mix_v, mixed_out, out_sem.at[4]).start()

    stats = st2[...].T[0:8]
    f_tx[...] = stats
    f_rx[j] = stats

    def f_copy(d):
        return remote(f_tx, f_rx.at[j], fs_sem.at[d - 1], fr_sem.at[d - 1], at(y, tr, z_peer(d)))

    for d in range(1, nz):
        f_copy(d).start()
    for d in range(1, nz):
        source = lax.rem(j + nz - d, nz)
        remote(f_tx, f_rx.at[source], fs_sem.at[d - 1], fr_sem.at[d - 1], here).wait_recv()
    total = f_rx[0]
    for z in range(1, nz):
        total = total + f_rx[z]
    flip[0:8] = total / width
    st2[...] = flip[...].T

    def last_step(t, carry):
        tile = st2[block_rows(t), :]
        rstd = ms[0, block_rows(t), :][:, 1:2]
        for q in range(nt):
            span = slice(q * quarter, (q + 1) * quarter)
            _, xhat = xhat_of(t, q)
            dn = ag_rx[t, q, 1].astype(F32)
            ig_v[block_rows(t), span] = (
                call[block_rows(t), span].astype(F32)
                + rstd * (dn - tile[:, 0:1] - xhat * tile[:, 1:2])
            ).astype(BF16)
        return carry

    lax.fori_loop(0, half, last_step, 0)
    pltpu.make_async_copy(ig_v, grad_out, out_sem.at[5]).start()

    for k, (rel, d) in enumerate(stat_list):
        stat_copy(k, rel, d).wait_send()
    y_cot.wait_send()
    y_tok.wait_send()

    def drain_block(s, carry):
        for k in range(2):
            inward(k, s)[0].wait_send()
            hbm_copy(k, s).wait()
        return carry

    lax.fori_loop(0, nb, drain_block, 0)

    @pl.when(is_mid)
    def _():
        def drain_out(s, carry):
            for k in range(2):
                outward(k, s).wait_send()
            return carry

        lax.fori_loop(0, nb, drain_out, 0)

    def drain_rows(t, carry):
        for d in range(1, nt):
            rs_copy(t, d).wait_send()
        return carry

    lax.fori_loop(0, ntb, drain_rows, 0)

    def drain_half(t, carry):
        yq_copy(t).wait_send()
        for d in range(1, nt):
            ag_copy(t, d).wait_send()
        return carry

    lax.fori_loop(0, half, drain_half, 0)
    for d in range(1, nz):
        f_copy(d).wait_send()
    pltpu.make_async_copy(mix_v, mixed_out, out_sem.at[4]).wait()
    pltpu.make_async_copy(ig_v, grad_out, out_sem.at[5]).wait()
    for rel, span in enumerate((own, far)):
        pltpu.make_async_copy(nall.at[span], norm_out.at[span], out_sem.at[rel]).wait()
        pltpu.make_async_copy(call.at[span], cot_out.at[span], out_sem.at[2 + rel]).wait()


def line_call(nz, nt, tokens, w_up, w_down, cotangent):
    rows, depth = tokens.shape
    ff = w_up.shape[1]
    tb, fb = 64, 512
    nfb = ff // fb
    ntb = 2 * rows // tb
    half = ntb // 2
    nb = nfb * ntb
    quarter = depth // nt
    vm = pltpu.VMEM
    dma = pltpu.SemaphoreType.DMA
    big = (2, nb, tb, fb)
    scratch = [
        vm((2 * rows, depth), BF16), vm((2 * rows, depth), BF16), vm((2 * rows, depth), BF16),
        vm((nfb, depth, fb), BF16), vm((nfb, fb, depth), BF16),
        vm(big, BF16), vm(big, BF16), vm(big, BF16), vm(big, BF16),
        vm((8, rows), F32), vm((2, nz, 8, rows), F32), vm((128, rows), F32), vm((2, rows, 128), F32),
        vm((2, tb, depth), F32),
        vm((ntb, nt - 1, 2, tb, quarter), BF16), vm((ntb, nt - 1, 2, tb, quarter), BF16),
        vm((ntb, 2, tb, quarter), F32),
        vm((half, 2, tb, quarter), BF16), vm((half, 2, tb, quarter), BF16),
        vm((half, nt, 2, tb, quarter), BF16),
        vm((rows, depth), BF16), vm((rows, 128), F32),
        vm((8, rows), F32), vm((nz, 8, rows), F32), vm((rows, depth), BF16),
        dma((2,)), dma((nfb,)), dma((nfb,)),
        dma((2, nb)), dma((2, nb)), dma((2, nb)), dma((2, nb)), dma((2, nb)), dma((2, nb)),
        dma((2 * nz - 1,)), dma((2, nz)), dma((2,)), dma((2,)),
        dma((ntb, nt - 1)), dma((ntb, nt - 1)), dma((half,)), dma((half,)),
        dma((half, nt - 1)), dma((half, nt - 1)),
        dma((nz - 1,)), dma((nz - 1,)), dma((6,)),
    ]
    any_spec = pl.BlockSpec(memory_space=pl.ANY)
    out = lambda *shape: jax.ShapeDtypeStruct(shape, BF16)
    return pl.pallas_call(
        functools.partial(line_kernel, (nz, nt, rows, depth, ff, tb, fb)),
        out_shape=(
            out(rows, depth), out(rows, depth), out(2 * rows, ff), out(2 * rows, ff),
            out(2 * rows, depth), out(2 * rows, depth),
        ),
        in_specs=[any_spec] * 4,
        out_specs=[any_spec] * 6,
        scratch_shapes=scratch,
        compiler_params=pltpu.CompilerParams(
            collective_id=0, has_side_effects=True, vmem_limit_bytes=56 * 1024 * 1024
        ),
    )(tokens, w_up, w_down, cotangent)


def local_line(tokens, w_up, w_down, cotangent):
    nz = lax.axis_size("tcol")
    nt = lax.axis_size("trow")
    mixed, grad, hidden, dpre, normed, cot = line_call(nz, nt, tokens, w_up, w_down, cotangent)
    grad_down = contract(hidden, cot, 0, 0).astype(BF16)
    grad_up = contract(normed, dpre, 0, 0).astype(BF16)
    return mixed, grad, grad_up, grad_down


def local_plain(tokens, w_up, w_down, cotangent):
    width = tokens.shape[1] * lax.axis_size("tcol")
    input_float = tokens.astype(F32)
    cot_all = lax.all_gather(cotangent, "fsdp", axis=0, tiled=True)
    sum_one, sum_two = lax.psum(
        (jnp.sum(input_float, axis=1), jnp.sum(input_float * input_float, axis=1)), "tcol"
    )
    token_mean = sum_one / width
    var = sum_two / width - token_mean * token_mean
    inverse_stddev = lax.rsqrt(var + EPS)
    centered_scaled = (input_float - token_mean[:, None]) * inverse_stddev[:, None]
    normalized_rows = centered_scaled.astype(BF16)
    normed_all = lax.all_gather(normalized_rows, "fsdp", axis=0, tiled=True)
    dhid_part = contract(cot_all, w_down, 1, 1).astype(BF16)
    dhid = lax.psum_scatter(dhid_part, "tcol", scatter_dimension=0, tiled=True).astype(F32)
    pre_part = contract(normed_all, w_up, 1, 0).astype(BF16)
    pre = lax.psum_scatter(pre_part, "tcol", scatter_dimension=0, tiled=True).astype(F32)
    hidden = lax.all_gather(gelu_value(pre).astype(BF16), "tcol", axis=0, tiled=True)
    dpre = lax.all_gather((dhid * gelu_slope(pre)).astype(BF16), "tcol", axis=0, tiled=True)
    branch_part = contract(hidden, w_down, 1, 0).astype(BF16)
    branch = lax.psum_scatter(branch_part, "fsdp", scatter_dimension=0, tiled=True)
    branch = lax.psum(branch, "trow").astype(F32)
    mixed = (input_float + branch).astype(BF16)
    grad_down = contract(hidden, cot_all, 0, 0).astype(BF16)
    dnorm_part = contract(dpre, w_up, 1, 1).astype(BF16)
    dnorm = lax.psum_scatter(dnorm_part, "fsdp", scatter_dimension=0, tiled=True)
    normed_gradient = lax.psum(dnorm, "trow").astype(F32)
    grad_up = contract(normed_all, dpre, 0, 0).astype(BF16)
    mean_first, mean_second = lax.psum(
        (jnp.sum(normed_gradient, axis=1), jnp.sum(normed_gradient * centered_scaled, axis=1)),
        "tcol",
    )
    first_moment = mean_first / width
    second_moment = mean_second / width
    input_gradient = cotangent.astype(F32) + inverse_stddev[:, None] * (
        normed_gradient - first_moment[:, None] - centered_scaled * second_moment[:, None]
    )
    return (mixed, input_gradient.astype(BF16), grad_up, grad_down)


def solution(mesh):
    fits = mesh.shape["fsdp"] == 2 and mesh.shape["tcol"] == 4
    return jax.shard_map(
        local_line if fits else local_plain,
        mesh=mesh,
        in_specs=(
            P("fsdp", "tcol"),
            P("tcol", ("fsdp", "trow")),
            P(("fsdp", "trow"), "tcol"),
            P("fsdp", "tcol"),
        ),
        out_specs=(
            P("fsdp", "tcol"),
            P("fsdp", "tcol"),
            P("tcol", ("fsdp", "trow")),
            P(("fsdp", "trow"), "tcol"),
        ),
        check_vma=False,
    )
```

time: 360 us -> 147 us (0.41)
  waiting for transfers between devices: 276 us -> 0 us
  Pallas kernels: 0 us -> 134 us
  blocking collectives: 25.2 us -> 0 us
  matrix products: 33.5 us -> 10.9 us
  between operations: 13.9 us -> 0.67 us
  other arithmetic: 10.2 us -> 0 us
    pallas_call x0 -> x1, Pallas kernels: none -> 134 us  [line_call(): pl.pallas_call(functools.partial(line_kernel, (nz, nt, rows, depth, ff, t...]
    reduce_scatter x4 -> x0, waiting for transfers between devices: 125 us -> none  [the longest x1 45.6 us: local(): lax.psum_scatter(dhid_part, 'tcol', scatter_dimension=0, tiled=True)]
    all_gather x4 -> x0, waiting for transfers between devices: 120 us -> none  [the longest x1 44.4 us: local(): lax.all_gather(gelu_value(pre).astype(jnp.bfloat16), 'tcol', axis=0, tile...]
    psum x1 -> x0, waiting for transfers between devices: 29.9 us -> none  [local(): branch = lax.psum(branch, 'trow').astype(jnp.float32)]
    psum x2 -> x0, blocking collectives: 25.2 us -> none  [the longest x1 13.5 us: local(): lax.psum((jnp.sum(input_float, axis=1), jnp.sum(input_float * input_float...]
    dot_general x6 -> x2, matrix products: 33.5 us -> 10.9 us  [contract(): lax.dot_general(left, right, (((left_dim,), (right_dim,)), ((), ())), pre...]
    convert_element_type x3 -> x0, other arithmetic: 7.41 us -> none  [the longest x1 2.71 us: local(): (dhid * gelu_slope(pre)).astype(jnp.bfloat16)]
  transfers between devices with their start and end apart: 9 -> 0, of which waited for: 9 -> 0; matrix products, arithmetic and copies ran while one was open for 9% -> 0% of each run, Pallas kernels for 0% -> 0%
where the time goes in v1:
time: 147 us
  Pallas kernels  134 us (91%)
  matrix products  10.9 us (7%)
  local copies, waits for them, and re-layouts  1.6 us (1%)
    pallas_call x1, Pallas kernels, line_call(): pl.pallas_call(functools.partial(line_kernel, (nz, nt, rows, depth, ff, t...  134 us
    dot_general x2, matrix products, contract(): lax.dot_general(left, right, (((left_dim,), (right_dim,)), ((), ())), pre...  10.9 us

profile of v1, /device:TPU:0, one launch (start us, length us, event | category | flops | bytes accessed | tf_op | source)
XLA Modules:
  0.0 147.3 jit_solution(12121606540082758991)
XLA Ops:
  0.6 134.1 %shard_map.75 = (bf16[256,1024]{1,0:T(8,128)(2,1)}, bf16[256,1024]{1,0:T(8,128)(2,1)}, bf16[512,2048]{1,0:T(8,128)(2,1)}, bf16[512,2048]{1,0:T(8,128)(2,1)}, bf1...) custom-call(bf16[256,1024]{1,0:T(8,128)(2,1)} %tok_in.1, bf16[1024,2048]{1,0:T(8,128)(2,1)} %up_in.1, ...), custom_call_target="tpu_custom_call" | custom-call | tf_op jit(solution)/shard_map/pallas_call | solution.py:481
  134.8 0.0 copy-start.2
  134.8 0.0 copy-start.3
  134.8 6.5 %convolution_convert_fusion.1 = bf16[1024,2048]{1,0:T(8,128)(2,1)} fusion(bf16[512,1024]{1,0:T(8,128)(2,1)} %get-tuple-element.12, bf16[512,2048]{1,0:T(8,128)(2,1)} %get-tuple-element.13), kind=kOutput, calls=%fused_computation.1 | convolution fusion | flops 2149580800 | bytes 7340032 | tf_op jit(solution)/shard_map/dot_general | solution.py:31
  141.3 0.0 copy-done.2
  141.3 0.0 copy-done.3
  141.3 0.0 copy-start.1
  141.3 0.0 copy-start
  141.3 4.4 %convolution_convert_fusion = bf16[2048,1024]{1,0:T(8,128)(2,1)} fusion(bf16[512,2048]{1,0:T(8,128)(2,1)S(1)} %copy-done.2, bf16[512,1024]{1,0:T(8,128)(2,1)S(1)} %copy-done.3), kind=kOutput, calls=%fused_computation | convolution fusion | flops 2149580800 | bytes 7340032 | tf_op jit(solution)/shard_map/dot_general | solution.py:31
  145.7 0.0 copy-done.1
  145.7 0.8 copy.10
  146.5 0.0 copy-done
  146.5 0.8 copy.11
Async XLA Ops:
  134.8 6.5 %copy-start.2 = (bf16[512,2048]{1,0:T(8,128)(2,1)S(1)}, bf16[512,2048]{1,0:T(8,128)(2,1)}, u32[]{:S(2)}) copy-start(bf16[512,2048]{1,0:T(8,128)(2,1)} %get-tuple-element.14) | copy-start | bytes 6291460
  134.8 6.5 %copy-start.3 = (bf16[512,1024]{1,0:T(8,128)(2,1)S(1)}, bf16[512,1024]{1,0:T(8,128)(2,1)}, u32[]{:S(2)}) copy-start(bf16[512,1024]{1,0:T(8,128)(2,1)} %get-tuple-element.15) | copy-start | bytes 3145732
  141.3 4.4 %copy-start.1 = (bf16[256,1024]{1,0:T(8,128)(2,1)S(1)}, bf16[256,1024]{1,0:T(8,128)(2,1)}, u32[]{:S(2)}) copy-start(bf16[256,1024]{1,0:T(8,128)(2,1)} %get-tuple-element.20) | copy-start | bytes 1572868
  141.3 5.2 %copy-start = (bf16[256,1024]{1,0:T(8,128)(2,1)S(1)}, bf16[256,1024]{1,0:T(8,128)(2,1)}, u32[]{:S(2)}) copy-start(bf16[256,1024]{1,0:T(8,128)(2,1)} %get-tuple-element.21) | copy-start | bytes 1572868

commit v2 on v0

v2 whole, which is shorter than its diff:
```python
import functools

import jax
import jax.numpy as jnp
from jax import lax
from jax.experimental import pallas as pl
from jax.experimental.pallas import tpu as pltpu
from jax.sharding import PartitionSpec as P

MESH = pl.DeviceIdType.MESH
BF16 = jnp.bfloat16
F32 = jnp.float32
SQRT_HALF = 0.7071067811865476
INV_SQRT_2PI = 0.3989422804014327
EPS = 1e-05
END_LAG = 16
MID_LAG = 3
ROW_SHIFT = 5
FB_SIZE = 256
VMEM_LIMIT = 46 * 1024 * 1024
WRITE_LIMIT = 1024 * 1024
OUT = pltpu.VMEM


def gelu_value(pre):
    phi = 0.5 * (1.0 + jax.scipy.special.erf(pre * SQRT_HALF))
    return pre * phi


def gelu_slope(pre):
    phi = 0.5 * (1.0 + jax.scipy.special.erf(pre * SQRT_HALF))
    return phi + pre * jnp.exp(-0.5 * pre * pre) * INV_SQRT_2PI


def contract(left, right, left_dim, right_dim):
    return lax.dot_general(
        left, right, (((left_dim,), (right_dim,)), ((), ())), preferred_element_type=F32
    )


def line_kernel(
    sizes,
    tok_in, up_in, down_in, cot_in,
    mixed, grad, grad_up, grad_down,
    xall, call, nall, wu, wd, tx, rx, rm, hd,
    st_own, st_tx, st_rx, flip, ms, acc, rs_tx, rs_rx, keep, y_tx, y_rx, ag_rx, square, sq_tx, sq_rx,
    load_sem, wu_sem, wd_sem, tx_sem, rx_sem, rm_sem, hs_sem, hr_sem,
    ss_sem, sr_sem, ys_sem, yr_sem, rss_sem, rsr_sem, yqs_sem, yqr_sem, ags_sem, agr_sem,
    sqs_sem, sqr_sem,
):
    nz, nt, rows, depth, ff, tb_size, fb_size = sizes
    nfb = ff // fb_size
    ntb = 2 * rows // tb_size
    half = ntb // 2
    lead = half // 2
    nb = ntb * nfb
    quarter = depth // nt
    width = depth * nz
    y = lax.axis_index("fsdp")
    tr = lax.axis_index("trow")
    j = lax.axis_index("tcol")
    mid_low = nz // 2 - 1
    is_mid = jnp.logical_or(j == mid_low, j == mid_low + 1)
    is_end = jnp.logical_not(is_mid)
    inner = jnp.where(j <= mid_low, j + 1, j - 1)
    outer = jnp.where(j <= mid_low, jnp.maximum(j - 1, 0), jnp.minimum(j + 1, nz - 1))
    lag = jnp.where(is_mid, MID_LAG, END_LAG)
    other = 1 - y

    def at(yy, tt, jj):
        return {"fsdp": yy, "trow": tt, "tcol": jj}

    def remote(src, dst, send, recv, device):
        return pltpu.make_async_remote_copy(
            src_ref=src, dst_ref=dst, send_sem=send, recv_sem=recv,
            device_id=device, device_id_type=MESH,
        )

    def z_peer(d):
        return lax.rem(j + d, nz)

    def t_peer(d):
        return lax.rem(tr + d, nt)

    here = at(y, tr, j)

    def own_block(o):
        return o if o < lead else o + half

    def block_rows(t):
        return pl.ds(pl.multiple_of(t * tb_size, tb_size), tb_size)

    head = lead * tb_size
    spans = [(pl.ds(0, head), pl.ds(0, head)), (pl.ds(head, rows - head), pl.ds(head + rows, rows - head))]

    def own_load(which, part):
        source, dest = (tok_in, xall) if which == 0 else (cot_in, call)
        return pltpu.make_async_copy(
            source.at[spans[part][0]], dest.at[spans[part][1]], load_sem.at[which, part]
        )

    def wd_load(f):
        return pltpu.make_async_copy(
            down_in.at[pl.ds(pl.multiple_of(f * fb_size, fb_size), fb_size)], wd.at[f], wd_sem.at[f]
        )

    def wu_load(f):
        return pltpu.make_async_copy(
            up_in.at[:, pl.ds(pl.multiple_of(f * fb_size, fb_size), fb_size)], wu.at[f], wu_sem.at[f]
        )

    for part in range(2):
        own_load(0, part).start()
    for part in range(2):
        own_load(1, part).start()
    for f in range(nfb):
        wd_load(f).start()
        wu_load(f).start()

    barrier = pltpu.get_barrier_semaphore()
    partners = [(y, t_peer(a), z_peer(b)) for a in range(nt) for b in range(nz) if a or b]
    partners += [(other, tr, z_peer(b)) for b in range(nz)]
    for device in partners:
        pl.semaphore_signal(barrier, inc=1, device_id=at(*device), device_id_type=MESH)

    lane = lax.broadcasted_iota(jnp.int32, (tb_size, 128), 1)

    def pair_tile(one, two):
        return jnp.where(lane == 0, one, jnp.where(lane == 1, two, 0.0))

    for part in range(2):
        own_load(0, part).wait()
    for o in range(half):
        x = xall[pl.ds(own_block(o) * tb_size, tb_size), :].astype(F32)
        st_own[o * tb_size:(o + 1) * tb_size, :] = pair_tile(
            jnp.sum(x, axis=1, keepdims=True), jnp.sum(x * x, axis=1, keepdims=True)
        )
    stats = st_own[...].T[0:8]
    st_tx[...] = stats
    st_rx[j] = stats
    square[...] = jnp.zeros_like(square)
    sq_tx[...] = jnp.zeros_like(sq_tx)
    pl.semaphore_wait(barrier, len(partners))

    def stat_copy(rel, d):
        target = at(y if rel == 0 else other, tr, z_peer(d))
        return remote(st_tx, st_rx.at[rel * nz + j], ss_sem, sr_sem.at[rel, d], target)

    stat_list = [(0, d) for d in range(1, nz)] + [(1, d) for d in range(nz)]
    for rel, d in stat_list:
        stat_copy(rel, d).start()
    for part in range(2):
        own_load(1, part).wait()

    def y_copy(which, o):
        ref = xall if which == 0 else call
        return remote(
            ref.at[pl.ds(own_block(o) * tb_size, tb_size)], ref.at[pl.ds((lead + o) * tb_size, tb_size)],
            ys_sem.at[which], yr_sem.at[which, o], at(other, tr, j),
        )

    for o in range(half):
        y_copy(1, o).start()
        y_copy(0, o).start()

    def statistics(rel):
        for d in range(1 if rel == 0 else 0, nz):
            source = lax.rem(j + nz - d, nz)
            remote(st_tx, st_rx.at[rel * nz + source], ss_sem, sr_sem.at[rel, d], here).wait_recv()
        total = st_rx[rel * nz]
        for z in range(1, nz):
            total = total + st_rx[rel * nz + z]
        total = total / width
        mean = total[0:1]
        flip[...] = jnp.zeros_like(flip)
        flip[0:1] = mean
        flip[1:2] = lax.rsqrt(total[1:2] - mean * mean + EPS)
        back = flip[...].T
        if rel == 0:
            ms[0:head] = back[0:head]
            ms[head + rows:] = back[head:]
        else:
            ms[head:head + rows] = back

    def xhat_of(t, span):
        tile = ms[block_rows(t), :]
        x = xall[block_rows(t), span].astype(F32)
        return x, (x - tile[:, 0:1]) * tile[:, 1:2]

    def is_far(t):
        return jnp.logical_and(t >= lead, t < lead + half)

    def normalize(t):
        @pl.when(t == 0)
        def _():
            statistics(0)

        @pl.when(t == lead)
        def _():
            statistics(1)

        for o in range(half):
            @pl.when(t == lead + o)
            def _(o=o):
                y_copy(1, o).wait_recv()
                y_copy(0, o).wait_recv()

        nall[block_rows(t), :] = xhat_of(t, slice(None))[1].astype(BF16)

    def to_mid(s):
        return remote(tx.at[s], rx.at[s], tx_sem, rx_sem.at[s], at(y, tr, inner))

    def across(s):
        return remote(tx.at[s], rm.at[s], tx_sem, rm_sem.at[s], at(y, tr, inner))

    def outward(s):
        span = hd.at[:, lax.rem(s, nfb), block_rows(s // nfb)]
        return remote(span, span, hs_sem, hr_sem.at[s], at(y, tr, outer))

    def partial_stage(s):
        t = s // nfb
        f = lax.rem(s, nfb)

        @pl.when(s < nfb)
        def _():
            wd_load(f).wait()
            wu_load(f).wait()

        @pl.when(f == 0)
        def _():
            normalize(t)

        parts = (
            contract(call[block_rows(t), :], wd[f], 1, 1),
            contract(nall[block_rows(t), :], wu[f], 1, 0),
        )

        @pl.when(is_end)
        def _():
            for k in range(2):
                tx[s, k] = parts[k].astype(BF16)
            to_mid(s).start()

        @pl.when(is_mid)
        def _():
            to_mid(s).wait_recv()
            for k in range(2):
                tx[s, k] = (parts[k] + rx[s, k].astype(F32)).astype(BF16)
            across(s).start()

    def act_stage(e):
        across(e).wait_recv()
        f = lax.rem(e, nfb)
        t = e // nfb

        def step(i, carry):
            r = pl.ds(pl.multiple_of(i * 16, 16), 16)
            out = pl.ds(pl.multiple_of(t * tb_size + i * 16, 16), 16)
            dhid = tx[e, 0, r, :].astype(F32) + rm[e, 0, r, :].astype(F32)
            pre = tx[e, 1, r, :].astype(F32) + rm[e, 1, r, :].astype(F32)
            phi = 0.5 * (1.0 + lax.erf(pre * SQRT_HALF))
            slope = phi + pre * jnp.exp(-0.5 * pre * pre) * INV_SQRT_2PI
            hd[0, f, out, :] = (pre * phi).astype(BF16)
            hd[1, f, out, :] = (dhid * slope).astype(BF16)
            return carry

        lax.fori_loop(0, tb_size // 16, step, 0)
        outward(e).start()

    def rs_copy(t, d):
        return remote(
            rs_tx.at[t, d - 1], rs_rx.at[t, d - 1], rss_sem, rsr_sem.at[t, d - 1],
            at(y, t_peer(d), j),
        )

    def columns(q):
        return pl.ds(pl.multiple_of(q * quarter, quarter), quarter)

    def use_stage(e):
        f = lax.rem(e, nfb)
        t = e // nfb

        @pl.when(is_end)
        def _():
            outward(e).wait_recv()

        @pl.when(f == 0)
        def _():
            acc[...] = jnp.zeros_like(acc)

        acc[0] += contract(hd[0, f, block_rows(t), :], wd[f], 1, 0)
        acc[1] += contract(hd[1, f, block_rows(t), :], wu[f], 1, 1)

        @pl.when(f == nfb - 1)
        def _():
            for d in range(1, nt):
                for k in range(2):
                    rs_tx[t, d - 1, k] = acc[k, :, columns(t_peer(d))].astype(BF16)
                rs_copy(t, d).start()
            for k in range(2):
                keep[t, k] = acc[k, :, columns(tr)]

    def first_rows(f, which):
        cols = pl.ds(pl.multiple_of(f * fb_size, fb_size), fb_size)
        if which == 0:
            grad_down[cols, :] = contract(hd[0, f, 0:rows, :], call[0:rows, :], 0, 0).astype(BF16)
        else:
            grad_up[:, cols] = contract(nall[0:rows, :], hd[1, f, 0:rows, :], 0, 0).astype(BF16)

    def last_rows(f, which):
        cols = pl.ds(pl.multiple_of(f * fb_size, fb_size), fb_size)
        if which == 0:
            part = contract(hd[0, f, rows:, :], call[rows:, :], 0, 0)
            grad_down[cols, :] = (grad_down[cols, :].astype(F32) + part).astype(BF16)
        else:
            part = contract(nall[rows:, :], hd[1, f, rows:, :], 0, 0)
            grad_up[:, cols] = (grad_up[:, cols].astype(F32) + part).astype(BF16)

    def yq_copy(o):
        return remote(y_tx.at[o], y_rx.at[o], yqs_sem, yqr_sem.at[o], at(other, tr, j))

    def ag_copy(o, d):
        return remote(
            ag_rx.at[o, tr], ag_rx.at[o, tr], ags_sem, agr_sem.at[o, d - 1],
            at(y, t_peer(d), j),
        )

    everyone = [(a, b) for a in range(nt) for b in range(nz) if a or b]

    def sq_copy(o, a, b):
        return remote(
            sq_tx.at[o], sq_rx.at[o, a * nz + b], sqs_sem, sqr_sem.at[o],
            at(y, t_peer(a), z_peer(b)),
        )

    def sq_all(o):
        span = sq_rx.at[o, pl.ds(1, nt * nz - 1)]
        return remote(span, span, sqs_sem, sqr_sem.at[o], here)

    def row_sum_stage(t):
        for d in range(1, nt):
            rs_copy(t, d).wait_recv()
        for k in range(2):
            total = keep[t, k]
            for d in range(1, nt):
                total = total + rs_rx[t, d - 1, k].astype(F32)
            keep[t, k] = total

        @pl.when(is_far(t))
        def _():
            for k in range(2):
                y_tx[t - lead, k] = keep[t, k].astype(BF16)
            yq_copy(t - lead).start()

    def gather_stage(o):
        t = jnp.where(o < lead, o, o + half)
        yq_copy(o).wait_recv()
        for k in range(2):
            ag_rx[o, tr, k] = (keep[t, k] + y_rx[o, k].astype(F32)).astype(BF16)
        for d in range(1, nt):
            ag_copy(o, d).start()
        dn = ag_rx[o, tr, 1].astype(F32)
        xhat = xhat_of(t, columns(tr))[1]
        square[0, 0:tb_size] = pair_tile(
            jnp.sum(dn, axis=1, keepdims=True), jnp.sum(dn * xhat, axis=1, keepdims=True)
        )
        sums = square[0].T[0:8]
        sq_tx[o] = sums
        sq_rx[o, 0] = sums
        for a, b in everyone:
            sq_copy(o, a, b).start()

    def finish_stage(o):
        t = jnp.where(o < lead, o, o + half)
        for d in range(1, nt):
            source = lax.rem(tr + nt - d, nt)
            remote(
                ag_rx.at[o, source], ag_rx.at[o, source], ags_sem,
                agr_sem.at[o, d - 1], here,
            ).wait_recv()
        sq_all(o).wait_recv()
        total = sq_rx[o, 0]
        for k in range(1, nt * nz):
            total = total + sq_rx[o, k]
        square[1, 0:8] = total / width
        means = square[1].T[0:tb_size]
        rstd = ms[block_rows(t), :][:, 1:2]
        for q in range(nt):
            span = slice(q * quarter, (q + 1) * quarter)
            x, xhat = xhat_of(t, span)
            mixed[block_rows(o), span] = (x + ag_rx[o, q, 0].astype(F32)).astype(BF16)
            dn = ag_rx[o, q, 1].astype(F32)
            grad[block_rows(o), span] = (
                call[block_rows(t), span].astype(F32)
                + rstd * (dn - means[:, 0:1] - xhat * means[:, 1:2])
            ).astype(BF16)

    pieces = 2 * nfb
    spread = nb // 2 // pieces

    def step(s, carry):
        @pl.when(s < nb)
        def _():
            with jax.named_scope("partial"):
                partial_stage(s)

        e = s - lag
        valid = jnp.logical_and(e >= 0, e < nb)

        @pl.when(jnp.logical_and(valid, is_mid))
        def _():
            with jax.named_scope("act"):
                act_stage(e)

        @pl.when(valid)
        def _():
            with jax.named_scope("use"):
                use_stage(e)

        g = e - nb // 2

        @pl.when(jnp.logical_and(g >= 0, jnp.logical_and(g < nb // 2, lax.rem(g, spread) == 0)))
        def _():
            with jax.named_scope("first"):
                p = g // spread

                @pl.when(p < nfb)
                def _():
                    first_rows(p, 0)

                @pl.when(p >= nfb)
                def _():
                    first_rows(p - nfb, 1)

        def done_block(shift, stage):
            k = e - shift - (nfb - 1)
            t = k // nfb

            @pl.when(jnp.logical_and(jnp.logical_and(k >= 0, t < ntb - 1), lax.rem(k, nfb) == 0))
            def _():
                stage(t)

        def gather_at(t):
            first = jnp.logical_and(t > lead, t <= half)

            @pl.when(jnp.logical_or(first, t >= half + lead))
            def _():
                with jax.named_scope("gather"):
                    gather_stage(jnp.where(first, t - lead - 1, t - half))

        done_block(ROW_SHIFT, row_sum_stage)
        done_block(ROW_SHIFT + 1, gather_at)
        return carry

    lax.fori_loop(0, nb + max(END_LAG, MID_LAG), step, 0)

    def last_piece(which):
        def body(f, carry):
            last_rows(f, which)
            return carry

        lax.fori_loop(0, nfb, body, 0)

    def finish_step(o, carry):
        finish_stage(o)
        return carry

    with jax.named_scope("last_down"):
        last_piece(0)
    with jax.named_scope("rowsum"):
        row_sum_stage(ntb - 1)
    with jax.named_scope("gather"):
        gather_stage(half - 1)
    with jax.named_scope("last_up"):
        last_piece(1)
    with jax.named_scope("finish"):
        lax.fori_loop(0, half, finish_step, 0)

    def sent(ref, sem):
        remote(ref, ref, sem, sem, here).wait_send()

    sent(st_rx.at[pl.ds(1, 2 * nz - 1)], ss_sem)
    far = pl.ds(head, rows)
    sent(xall.at[far], ys_sem.at[0])
    sent(call.at[far], ys_sem.at[1])
    sent(tx, tx_sem)

    @pl.when(is_mid)
    def _():
        sent(hd, hs_sem)

    sent(rs_tx, rss_sem)
    sent(y_tx, yqs_sem)
    sent(ag_rx.at[:, pl.ds(0, nt - 1)], ags_sem)
    sent(sq_rx.at[:, pl.ds(1, nt * nz - 1)], sqs_sem)


def line_call(nz, nt, tokens, w_up, w_down, cotangent):
    rows, depth = tokens.shape
    ff = w_up.shape[1]
    tb, fb = 64, FB_SIZE
    nfb = ff // fb
    ntb = 2 * rows // tb
    half = ntb // 2
    nb = nfb * ntb
    quarter = depth // nt
    vm = pltpu.VMEM
    dma = pltpu.SemaphoreType.DMA
    big = (nb, 2, tb, fb)
    scratch = [
        vm((2 * rows, depth), BF16), vm((2 * rows, depth), BF16), vm((2 * rows, depth), BF16),
        vm((nfb, depth, fb), BF16), vm((nfb, fb, depth), BF16),
        vm(big, BF16), vm(big, BF16), vm(big, BF16), vm((2, nfb, 2 * rows, fb), BF16),
        vm((rows, 128), F32), vm((8, rows), F32), vm((2 * nz, 8, rows), F32), vm((128, rows), F32),
        vm((2 * rows, 128), F32),
        vm((2, tb, depth), F32),
        vm((ntb, nt - 1, 2, tb, quarter), BF16), vm((ntb, nt - 1, 2, tb, quarter), BF16),
        vm((ntb, 2, tb, quarter), F32),
        vm((half, 2, tb, quarter), BF16), vm((half, 2, tb, quarter), BF16),
        vm((half, nt, 2, tb, quarter), BF16),
        vm((2, 128, 128), F32), vm((half, 8, 128), F32), vm((half, nt * nz, 8, 128), F32),
        dma((2, 2)), dma((nfb,)), dma((nfb,)),
        dma, dma((nb,)), dma((nb,)), dma, dma((nb,)),
        dma, dma((2, nz)), dma((2,)), dma((2, half)),
        dma, dma((ntb, nt - 1)), dma, dma((half,)),
        dma, dma((half, nt - 1)), dma, dma((half,)),
    ]
    return pl.pallas_call(
        functools.partial(line_kernel, (nz, nt, rows, depth, ff, tb, fb)),
        out_shape=tuple(
            OUT(shape, BF16)
            for shape in ((rows, depth), (rows, depth), (depth, ff), (ff, depth))
        ),
        in_specs=[pl.BlockSpec(memory_space=pl.ANY)] * 4,
        out_specs=[pl.BlockSpec(memory_space=pltpu.VMEM)] * 4,
        scratch_shapes=scratch,
        compiler_params=pltpu.CompilerParams(
            collective_id=0, has_side_effects=True, vmem_limit_bytes=VMEM_LIMIT
        ),
    )(tokens, w_up, w_down, cotangent)


def write_kernel(*refs):
    n = len(refs) // 2
    sems = refs[-1]
    copies = []
    for k in range(n):
        rows = refs[k].shape[0]
        cuts = 4 if rows * refs[k].shape[1] > 1 << 20 else 1
        for c in range(cuts):
            span = pl.ds(c * (rows // cuts), rows // cuts)
            copies.append((refs[k].at[span], refs[n + k].at[span]))
    copies = [pltpu.make_async_copy(a, b, sems.at[i]) for i, (a, b) in enumerate(copies)]
    for copy in copies:
        copy.start()
    for copy in copies:
        copy.wait()


def write_out(arrays):
    return pl.pallas_call(
        write_kernel,
        out_shape=tuple(jax.ShapeDtypeStruct(a.shape, a.dtype) for a in arrays),
        in_specs=[pl.BlockSpec(memory_space=pltpu.VMEM)] * len(arrays),
        out_specs=[pl.BlockSpec(memory_space=pl.ANY)] * len(arrays),
        scratch_shapes=[pltpu.SemaphoreType.DMA((16,))],
        compiler_params=pltpu.CompilerParams(vmem_limit_bytes=WRITE_LIMIT),
    )(*arrays)


def local_line(tokens, w_up, w_down, cotangent):
    nz = lax.axis_size("tcol")
    nt = lax.axis_size("trow")
    return write_out(line_call(nz, nt, tokens, w_up, w_down, cotangent))


def local_plain(tokens, w_up, w_down, cotangent):
    width = tokens.shape[1] * lax.axis_size("tcol")
    input_float = tokens.astype(F32)
    cot_all = lax.all_gather(cotangent, "fsdp", axis=0, tiled=True)
    sum_one, sum_two = lax.psum(
        (jnp.sum(input_float, axis=1), jnp.sum(input_float * input_float, axis=1)), "tcol"
    )
    token_mean = sum_one / width
    var = sum_two / width - token_mean * token_mean
    inverse_stddev = lax.rsqrt(var + EPS)
    centered_scaled = (input_float - token_mean[:, None]) * inverse_stddev[:, None]
    normalized_rows = centered_scaled.astype(BF16)
    normed_all = lax.all_gather(normalized_rows, "fsdp", axis=0, tiled=True)
    dhid_part = contract(cot_all, w_down, 1, 1).astype(BF16)
    dhid = lax.psum_scatter(dhid_part, "tcol", scatter_dimension=0, tiled=True).astype(F32)
    pre_part = contract(normed_all, w_up, 1, 0).astype(BF16)
    pre = lax.psum_scatter(pre_part, "tcol", scatter_dimension=0, tiled=True).astype(F32)
    hidden = lax.all_gather(gelu_value(pre).astype(BF16), "tcol", axis=0, tiled=True)
    dpre = lax.all_gather((dhid * gelu_slope(pre)).astype(BF16), "tcol", axis=0, tiled=True)
    branch_part = contract(hidden, w_down, 1, 0).astype(BF16)
    branch = lax.psum_scatter(branch_part, "fsdp", scatter_dimension=0, tiled=True)
    branch = lax.psum(branch, "trow").astype(F32)
    mixed = (input_float + branch).astype(BF16)
    grad_down = contract(hidden, cot_all, 0, 0).astype(BF16)
    dnorm_part = contract(dpre, w_up, 1, 1).astype(BF16)
    dnorm = lax.psum_scatter(dnorm_part, "fsdp", scatter_dimension=0, tiled=True)
    normed_gradient = lax.psum(dnorm, "trow").astype(F32)
    grad_up = contract(normed_all, dpre, 0, 0).astype(BF16)
    mean_first, mean_second = lax.psum(
        (jnp.sum(normed_gradient, axis=1), jnp.sum(normed_gradient * centered_scaled, axis=1)),
        "tcol",
    )
    first_moment = mean_first / width
    second_moment = mean_second / width
    input_gradient = cotangent.astype(F32) + inverse_stddev[:, None] * (
        normed_gradient - first_moment[:, None] - centered_scaled * second_moment[:, None]
    )
    return (mixed, input_gradient.astype(BF16), grad_up, grad_down)


def solution(mesh):
    fits = mesh.shape["fsdp"] == 2 and mesh.shape["tcol"] == 4
    return jax.shard_map(
        local_line if fits else local_plain,
        mesh=mesh,
        in_specs=(
            P("fsdp", "tcol"),
            P("tcol", ("fsdp", "trow")),
            P(("fsdp", "trow"), "tcol"),
            P("fsdp", "tcol"),
        ),
        out_specs=(
            P("fsdp", "tcol"),
            P("fsdp", "tcol"),
            P("tcol", ("fsdp", "trow")),
            P(("fsdp", "trow"), "tcol"),
        ),
        check_vma=False,
    )
```

time: 360 us -> 129 us (0.36)
  waiting for transfers between devices: 276 us -> 0 us
  Pallas kernels: 0 us -> 129 us
  matrix products: 33.5 us -> 0 us
  blocking collectives: 25.2 us -> 0 us
  between operations: 13.9 us -> 0.64 us
  other arithmetic: 10.2 us -> 0 us
    pallas_call x0 -> x2, Pallas kernels: none -> 129 us  [the longest x1 125 us: line_call(): pl.pallas_call(functools.partial(line_kernel, (nz, nt, rows, depth, ff, t...]
    reduce_scatter x4 -> x0, waiting for transfers between devices: 125 us -> none  [the longest x1 45.6 us: local(): lax.psum_scatter(dhid_part, 'tcol', scatter_dimension=0, tiled=True)]
    all_gather x4 -> x0, waiting for transfers between devices: 120 us -> none  [the longest x1 44.4 us: local(): lax.all_gather(gelu_value(pre).astype(jnp.bfloat16), 'tcol', axis=0, tile...]
    dot_general x6 -> x0, matrix products: 33.5 us -> none  [contract(): lax.dot_general(left, right, (((left_dim,), (right_dim,)), ((), ())), pre...]
    psum x1 -> x0, waiting for transfers between devices: 29.9 us -> none  [local(): branch = lax.psum(branch, 'trow').astype(jnp.float32)]
    psum x2 -> x0, blocking collectives: 25.2 us -> none  [the longest x1 13.5 us: local(): lax.psum((jnp.sum(input_float, axis=1), jnp.sum(input_float * input_float...]
    convert_element_type x3 -> x0, other arithmetic: 7.41 us -> none  [the longest x1 2.71 us: local(): (dhid * gelu_slope(pre)).astype(jnp.bfloat16)]
  transfers between devices with their start and end apart: 9 -> 0, of which waited for: 9 -> 0; matrix products, arithmetic and copies ran while one was open for 9% -> 0% of each run, Pallas kernels for 0% -> 0%
where the time goes in v2:
time: 129 us
  Pallas kernels  129 us (100%)
    pallas_call x1, Pallas kernels, line_call(): pl.pallas_call(functools.partial(line_kernel, (nz, nt, rows, depth, ff, t...  125 us
    pallas_call x1, Pallas kernels, write_out(): pl.pallas_call(write_kernel, out_shape=tuple((jax.ShapeDtypeStruct(a.shap...  3.76 us

profile of v2, /device:TPU:0, one launch (start us, length us, event | category | flops | bytes accessed | tf_op | source)
XLA Modules:
  0.0 129.2 jit_solution(5546743342434040401)
XLA Ops:
  0.6 124.8 %shard_map.75 = (bf16[256,1024]{1,0:T(8,128)(2,1)S(1)}, bf16[256,1024]{1,0:T(8,128)(2,1)S(1)}, bf16[1024,2048]{1,0:T(8,128)(2,1)S(1)}, bf16[2048,1024]{1,0:T(8,128)(2,1)S(1)}) custom-call(bf16[256,1024]{1,0:T(8,128)(2,1)} %tok_in.1, bf16[1024,2048]{1,0:T(8,128)(2,1)} %up_in.1, bf16[2048,1024]{1,0:T(8,128)(2,1)} %down_in.1, bf16[256,1024]{1,0:T(8,128)(2,1)} %cot_in.1), custom_call_target="tpu_custom_call" | custom-call | tf_op jit(solution)/shard_map/pallas_call | solution.py:528
  125.4 3.8 %shard_map.76 = (bf16[256,1024]{1,0:T(8,128)(2,1)}, bf16[256,1024]{1,0:T(8,128)(2,1)}, bf16[1024,2048]{1,0:T(8,128)(2,1)}, bf16[2048,1024]{1,0:T(8,128)(2,1)}) custom-call(bf16[256,1024]{1,0:T(8,128)(2,1)S(1)} %get-tuple-element.8.refs_0_, bf16[256,1024]{1,0:T(8,128)(2,1)S(1)} %get-tuple-element.9.refs_1_, bf16[1024,2048]{1,0:T(8,128)(2,1)S(1)} %get-tuple-element.10.refs_2_, ...), custom_call_target="tpu_custom_call" | custom-call | tf_op jit(solution)/shard_map/pallas_call | solution.py:561

commit v3 on v2

--- a/solution.py
+++ b/solution.py
@@ -13,9 +13,14 @@
 SQRT_HALF = 0.7071067811865476
 INV_SQRT_2PI = 0.3989422804014327
 EPS = 1e-05
-END_LAG = 16
+END_LAG = 12
 MID_LAG = 3
 ROW_SHIFT = 5
+RING = 15
+MID_RING = 10
+COLS_AT = 3
+CUTS = 4
+SUMS_AT = 1
 FB_SIZE = 256
 VMEM_LIMIT = 46 * 1024 * 1024
 WRITE_LIMIT = 1024 * 1024
@@ -42,11 +47,11 @@
     sizes,
     tok_in, up_in, down_in, cot_in,
     mixed, grad, grad_up, grad_down,
-    xall, call, nall, wu, wd, tx, rx, rm, hd,
+    xall, call, nall, cs_tx, cs_rx, wu, wd, tx, rx, rm, hd,
     st_own, st_tx, st_rx, flip, ms, acc, rs_tx, rs_rx, keep, y_tx, y_rx, ag_rx, square, sq_tx, sq_rx,
     load_sem, wu_sem, wd_sem, tx_sem, rx_sem, rm_sem, hs_sem, hr_sem,
     ss_sem, sr_sem, ys_sem, yr_sem, rss_sem, rsr_sem, yqs_sem, yqr_sem, ags_sem, agr_sem,
-    sqs_sem, sqr_sem,
+    sqs_sem, sqr_sem, css_sem, csr_sem,
 ):
     nz, nt, rows, depth, ff, tb_size, fb_size = sizes
     nfb = ff // fb_size
@@ -62,6 +67,7 @@
     mid_low = nz // 2 - 1
     is_mid = jnp.logical_or(j == mid_low, j == mid_low + 1)
     is_end = jnp.logical_not(is_mid)
+    is_odd = lax.rem(tr, 2) == 1
     inner = jnp.where(j <= mid_low, j + 1, j - 1)
     outer = jnp.where(j <= mid_low, jnp.maximum(j - 1, 0), jnp.minimum(j + 1, nz - 1))
     lag = jnp.where(is_mid, MID_LAG, END_LAG)
@@ -109,13 +115,10 @@
             up_in.at[:, pl.ds(pl.multiple_of(f * fb_size, fb_size), fb_size)], wu.at[f], wu_sem.at[f]
         )
 
-    for part in range(2):
-        own_load(0, part).start()
-    for part in range(2):
-        own_load(1, part).start()
-    for f in range(nfb):
-        wd_load(f).start()
-        wu_load(f).start()
+    own_load(1, 0).start()
+    own_load(0, 0).start()
+    wd_load(0).start()
+    wu_load(0).start()
 
     barrier = pltpu.get_barrier_semaphore()
     partners = [(y, t_peer(a), z_peer(b)) for a in range(nt) for b in range(nz) if a or b]
@@ -128,29 +131,47 @@
     def pair_tile(one, two):
         return jnp.where(lane == 0, one, jnp.where(lane == 1, two, 0.0))
 
-    for part in range(2):
-        own_load(0, part).wait()
-    for o in range(half):
-        x = xall[pl.ds(own_block(o) * tb_size, tb_size), :].astype(F32)
-        st_own[o * tb_size:(o + 1) * tb_size, :] = pair_tile(
-            jnp.sum(x, axis=1, keepdims=True), jnp.sum(x * x, axis=1, keepdims=True)
-        )
-    stats = st_own[...].T[0:8]
-    st_tx[...] = stats
-    st_rx[j] = stats
+    own_load(0, 1).start()
+    for f in range(1, nfb):
+        wu_load(f).start()
+        wd_load(f).start()
+    own_load(1, 1).start()
     square[...] = jnp.zeros_like(square)
     sq_tx[...] = jnp.zeros_like(sq_tx)
+    own_load(1, 0).wait()
+    own_load(0, 0).wait()
+
+    x = xall[0:tb_size, :].astype(F32)
+    nall[0:tb_size, :] = (x - jnp.sum(x, axis=1, keepdims=True) / depth).astype(BF16)
+
+    def parts_of(t, f):
+        return (
+            contract(call[block_rows(t), :], wd[f], 1, 1),
+            contract(nall[block_rows(t), :], wu[f], 1, 0),
+        )
+
+    def to_mid(s):
+        return remote(tx.at[s], rx.at[s], tx_sem, rx_sem.at[lax.rem(s, RING)], at(y, tr, inner))
+
+    @pl.when(is_end)
+    def _():
+        wd_load(0).wait()
+        wu_load(0).wait()
+        parts = parts_of(0, 0)
+        for k in range(2):
+            tx[0, k] = parts[k].astype(BF16)
+
     pl.semaphore_wait(barrier, len(partners))
+
+    @pl.when(is_end)
+    def _():
+        to_mid(0).start()
 
     def stat_copy(rel, d):
         target = at(y if rel == 0 else other, tr, z_peer(d))
-        return remote(st_tx, st_rx.at[rel * nz + j], ss_sem, sr_sem.at[rel, d], target)
+        return remote(st_tx, st_rx.at[rel * nz + j], ss_sem, sr_sem.at[rel], target)
 
     stat_list = [(0, d) for d in range(1, nz)] + [(1, d) for d in range(nz)]
-    for rel, d in stat_list:
-        stat_copy(rel, d).start()
-    for part in range(2):
-        own_load(1, part).wait()
 
     def y_copy(which, o):
         ref = xall if which == 0 else call
@@ -159,14 +180,51 @@
             ys_sem.at[which], yr_sem.at[which, o], at(other, tr, j),
         )
 
-    for o in range(half):
-        y_copy(1, o).start()
-        y_copy(0, o).start()
+    def cs_copy(z):
+        return remote(cs_tx, cs_rx.at[j], css_sem, csr_sem, at(y, tr, z))
+
+    mids = (mid_low, mid_low + 1)
+
+    def token_sums():
+        own_load(0, 1).wait()
+        for o in range(half):
+            x = xall[pl.ds(own_block(o) * tb_size, tb_size), :].astype(F32)
+            st_own[o * tb_size:(o + 1) * tb_size, :] = pair_tile(
+                jnp.sum(x, axis=1, keepdims=True), jnp.sum(x * x, axis=1, keepdims=True)
+            )
+        stats = st_own[...].T[0:2]
+        st_tx[...] = stats
+        st_rx[j] = stats
+        for rel, d in stat_list:
+            if rel == 0:
+                stat_copy(rel, d).start()
+
+    def column_sums(waited):
+        ones = jnp.ones((8, depth), BF16)
+        for f in range(nfb):
+            if f >= waited:
+                wu_load(f).wait()
+            cs_tx[f:f + 1] = contract(ones, wu[f], 1, 0)[0:1]
+        for z in mids:
+            @pl.when(j != z)
+            def _(z=z):
+                cs_copy(z).start()
+
+        @pl.when(is_mid)
+        def _():
+            cs_rx[j] = cs_tx[...]
+
+        for rel, d in stat_list:
+            if rel == 1:
+                stat_copy(rel, d).start()
+        own_load(1, 1).wait()
+        for o in range(half):
+            y_copy(1, o).start()
+            y_copy(0, o).start()
 
     def statistics(rel):
-        for d in range(1 if rel == 0 else 0, nz):
-            source = lax.rem(j + nz - d, nz)
-            remote(st_tx, st_rx.at[rel * nz + source], ss_sem, sr_sem.at[rel, d], here).wait_recv()
+        span = st_rx.at[pl.ds(rel * nz, nz - 1 + rel)]
+        remote(span, span, ss_sem, sr_sem.at[rel], here).wait_recv()
         total = st_rx[rel * nz]
         for z in range(1, nz):
             total = total + st_rx[rel * nz + z]
@@ -174,7 +232,10 @@
         mean = total[0:1]
         flip[...] = jnp.zeros_like(flip)
         flip[0:1] = mean
-        flip[1:2] = lax.rsqrt(total[1:2] - mean * mean + EPS)
+        rstd = lax.rsqrt(total[1:2] - mean * mean + EPS)
+        flip[1:2] = rstd
+        for z in range(nz):
+            flip[2 + z:3 + z] = rstd * (st_rx[rel * nz + z][0:1] / depth - mean)
         back = flip[...].T
         if rel == 0:
             ms[0:head] = back[0:head]
@@ -190,10 +251,21 @@
     def is_far(t):
         return jnp.logical_and(t >= lead, t < lead + half)
 
-    def normalize(t):
-        @pl.when(t == 0)
-        def _():
-            statistics(0)
+    def norm_rows(t):
+        nall[block_rows(t), :] = xhat_of(t, slice(None))[1].astype(BF16)
+
+    def first_statistics():
+        statistics(0)
+
+        @pl.when(is_mid)
+        def _():
+            span = cs_rx.at[pl.ds(0, nz - 1)]
+            remote(span, span, css_sem, csr_sem, here).wait_recv()
+
+    def make_rows(t):
+        @pl.when(t == 1)
+        def _():
+            norm_rows(0)
 
         @pl.when(t == lead)
         def _():
@@ -205,17 +277,16 @@
                 y_copy(1, o).wait_recv()
                 y_copy(0, o).wait_recv()
 
-        nall[block_rows(t), :] = xhat_of(t, slice(None))[1].astype(BF16)
-
-    def to_mid(s):
-        return remote(tx.at[s], rx.at[s], tx_sem, rx_sem.at[s], at(y, tr, inner))
+        @pl.when(t > 0)
+        def _():
+            norm_rows(t)
 
     def across(s):
-        return remote(tx.at[s], rm.at[s], tx_sem, rm_sem.at[s], at(y, tr, inner))
+        return remote(tx.at[s], rm.at[s], tx_sem, rm_sem.at[lax.rem(s, MID_RING)], at(y, tr, inner))
 
     def outward(s):
         span = hd.at[:, lax.rem(s, nfb), block_rows(s // nfb)]
-        return remote(span, span, hs_sem, hr_sem.at[s], at(y, tr, outer))
+        return remote(span, span, hs_sem, hr_sem.at[lax.rem(s, RING)], at(y, tr, outer))
 
     def partial_stage(s):
         t = s // nfb
@@ -224,16 +295,12 @@
         @pl.when(s < nfb)
         def _():
             wd_load(f).wait()
-            wu_load(f).wait()
 
         @pl.when(f == 0)
         def _():
-            normalize(t)
-
-        parts = (
-            contract(call[block_rows(t), :], wd[f], 1, 1),
-            contract(nall[block_rows(t), :], wu[f], 1, 0),
-        )
+            make_rows(t)
+
+        parts = parts_of(t, f)
 
         @pl.when(is_end)
         def _():
@@ -253,23 +320,32 @@
         f = lax.rem(e, nfb)
         t = e // nfb
 
-        def step(i, carry):
+        def step(first, i, carry):
             r = pl.ds(pl.multiple_of(i * 16, 16), 16)
             out = pl.ds(pl.multiple_of(t * tb_size + i * 16, 16), 16)
             dhid = tx[e, 0, r, :].astype(F32) + rm[e, 0, r, :].astype(F32)
             pre = tx[e, 1, r, :].astype(F32) + rm[e, 1, r, :].astype(F32)
+            if first:
+                tile = ms[out, :]
+                pre = pre * tile[:, 1:2]
+                for z in range(nz):
+                    pre = pre + tile[:, 2 + z:3 + z] * cs_rx[z, pl.ds(f, 1), :]
             phi = 0.5 * (1.0 + lax.erf(pre * SQRT_HALF))
             slope = phi + pre * jnp.exp(-0.5 * pre * pre) * INV_SQRT_2PI
             hd[0, f, out, :] = (pre * phi).astype(BF16)
             hd[1, f, out, :] = (dhid * slope).astype(BF16)
             return carry
 
-        lax.fori_loop(0, tb_size // 16, step, 0)
+        for first in (True, False):
+            @pl.when((e < nfb) == first)
+            def _(first=first):
+                lax.fori_loop(0, tb_size // 16, functools.partial(step, first), 0)
+
         outward(e).start()
 
-    def rs_copy(t, d):
+    def rs_copy(t, d, k):
         return remote(
-            rs_tx.at[t, d - 1], rs_rx.at[t, d - 1], rss_sem, rsr_sem.at[t, d - 1],
+            rs_tx.at[t, d - 1, k], rs_rx.at[t, d - 1, k], rss_sem, rsr_sem.at[t],
             at(y, t_peer(d), j),
         )
 
@@ -288,17 +364,18 @@
         def _():
             acc[...] = jnp.zeros_like(acc)
 
+        def summed(k):
+            @pl.when(f == nfb - 1)
+            def _():
+                for d in range(1, nt):
+                    rs_tx[t, d - 1, k] = acc[k, :, columns(t_peer(d))].astype(BF16)
+                    rs_copy(t, d, k).start()
+                keep[t, k] = acc[k, :, columns(tr)]
+
         acc[0] += contract(hd[0, f, block_rows(t), :], wd[f], 1, 0)
         acc[1] += contract(hd[1, f, block_rows(t), :], wu[f], 1, 1)
-
-        @pl.when(f == nfb - 1)
-        def _():
-            for d in range(1, nt):
-                for k in range(2):
-                    rs_tx[t, d - 1, k] = acc[k, :, columns(t_peer(d))].astype(BF16)
-                rs_copy(t, d).start()
-            for k in range(2):
-                keep[t, k] = acc[k, :, columns(tr)]
+        summed(0)
+        summed(1)
 
     def first_rows(f, which):
         cols = pl.ds(pl.multiple_of(f * fb_size, fb_size), fb_size)
@@ -319,9 +396,9 @@
     def yq_copy(o):
         return remote(y_tx.at[o], y_rx.at[o], yqs_sem, yqr_sem.at[o], at(other, tr, j))
 
-    def ag_copy(o, d):
+    def ag_copy(o, d, k):
         return remote(
-            ag_rx.at[o, tr], ag_rx.at[o, tr], ags_sem, agr_sem.at[o, d - 1],
+            ag_rx.at[o, tr, k], ag_rx.at[o, tr, k], ags_sem, agr_sem.at[o],
             at(y, t_peer(d), j),
         )
 
@@ -338,8 +415,7 @@
         return remote(span, span, sqs_sem, sqr_sem.at[o], here)
 
     def row_sum_stage(t):
-        for d in range(1, nt):
-            rs_copy(t, d).wait_recv()
+        remote(rs_tx.at[t], rs_rx.at[t], rss_sem, rsr_sem.at[t], here).wait_recv()
         for k in range(2):
             total = keep[t, k]
             for d in range(1, nt):
@@ -357,32 +433,31 @@
         yq_copy(o).wait_recv()
         for k in range(2):
             ag_rx[o, tr, k] = (keep[t, k] + y_rx[o, k].astype(F32)).astype(BF16)
-        for d in range(1, nt):
-            ag_copy(o, d).start()
+            if k == 0:
+                for d in range(1, nt):
+                    ag_copy(o, d, k).start()
         dn = ag_rx[o, tr, 1].astype(F32)
         xhat = xhat_of(t, columns(tr))[1]
         square[0, 0:tb_size] = pair_tile(
             jnp.sum(dn, axis=1, keepdims=True), jnp.sum(dn * xhat, axis=1, keepdims=True)
         )
-        sums = square[0].T[0:8]
+        sums = square[0].T[0:2]
         sq_tx[o] = sums
         sq_rx[o, 0] = sums
         for a, b in everyone:
             sq_copy(o, a, b).start()
+        for d in range(1, nt):
+            ag_copy(o, d, 1).start()
 
     def finish_stage(o):
         t = jnp.where(o < lead, o, o + half)
-        for d in range(1, nt):
-            source = lax.rem(tr + nt - d, nt)
-            remote(
-                ag_rx.at[o, source], ag_rx.at[o, source], ags_sem,
-                agr_sem.at[o, d - 1], here,
-            ).wait_recv()
+        span = ag_rx.at[o, pl.ds(0, nt - 1)]
+        remote(span, span, ags_sem, agr_sem.at[o], here).wait_recv()
         sq_all(o).wait_recv()
         total = sq_rx[o, 0]
         for k in range(1, nt * nz):
             total = total + sq_rx[o, k]
-        square[1, 0:8] = total / width
+        square[1, 0:2] = total / width
         means = square[1].T[0:tb_size]
         rstd = ms[block_rows(t), :][:, 1:2]
         for q in range(nt):
@@ -399,13 +474,47 @@
     spread = nb // 2 // pieces
 
     def step(s, carry):
-        @pl.when(s < nb)
+        @pl.when(jnp.logical_and(s == 0, jnp.logical_or(is_mid, is_odd)))
+        def _():
+            with jax.named_scope("sums"):
+                token_sums()
+
+        @pl.when(jnp.logical_and(s == 0, is_mid))
+        def _():
+            with jax.named_scope("cols"):
+                column_sums(0)
+
+        @pl.when(jnp.logical_and(jnp.logical_and(s > 0, s <= COLS_AT), is_end))
+        def _():
+            wu_load(s).wait()
+
+        @pl.when(jnp.logical_and(s == nfb, is_end))
+        def _():
+            with jax.named_scope("norm"):
+                first_statistics()
+
+        @pl.when(jnp.logical_and(s < nb, jnp.logical_or(is_mid, s > 0)))
         def _():
             with jax.named_scope("partial"):
                 partial_stage(s)
 
+        @pl.when(jnp.logical_and(s == SUMS_AT, jnp.logical_and(is_end, jnp.logical_not(is_odd))))
+        def _():
+            with jax.named_scope("sums"):
+                token_sums()
+
+        @pl.when(jnp.logical_and(s == COLS_AT, is_end))
+        def _():
+            with jax.named_scope("cols"):
+                column_sums(COLS_AT + 1)
+
         e = s - lag
         valid = jnp.logical_and(e >= 0, e < nb)
+
+        @pl.when(jnp.logical_and(e == 0, is_mid))
+        def _():
+            with jax.named_scope("norm"):
+                first_statistics()
 
         @pl.when(jnp.logical_and(valid, is_mid))
         def _():
@@ -479,11 +588,21 @@
     def sent(ref, sem):
         remote(ref, ref, sem, sem, here).wait_send()
 
-    sent(st_rx.at[pl.ds(1, 2 * nz - 1)], ss_sem)
+    with jax.named_scope("drain"):
+        sent(st_rx.at[pl.ds(1, 2 * nz - 1)], ss_sem)
     far = pl.ds(head, rows)
     sent(xall.at[far], ys_sem.at[0])
     sent(call.at[far], ys_sem.at[1])
     sent(tx, tx_sem)
+
+    @pl.when(is_end)
+    def _():
+        sent(cs_rx.at[pl.ds(0, 2)], css_sem)
+
+    @pl.when(is_mid)
+    def _():
+        sent(cs_rx.at[0], css_sem)
+
 
     @pl.when(is_mid)
     def _():
@@ -504,26 +623,28 @@
     half = ntb // 2
     nb = nfb * ntb
     quarter = depth // nt
+    sums = -(-nfb // 8) * 8
     vm = pltpu.VMEM
     dma = pltpu.SemaphoreType.DMA
     big = (nb, 2, tb, fb)
     scratch = [
         vm((2 * rows, depth), BF16), vm((2 * rows, depth), BF16), vm((2 * rows, depth), BF16),
+        vm((sums, fb), F32), vm((nz, sums, fb), F32),
         vm((nfb, depth, fb), BF16), vm((nfb, fb, depth), BF16),
         vm(big, BF16), vm(big, BF16), vm(big, BF16), vm((2, nfb, 2 * rows, fb), BF16),
-        vm((rows, 128), F32), vm((8, rows), F32), vm((2 * nz, 8, rows), F32), vm((128, rows), F32),
+        vm((rows, 128), F32), vm((2, rows), F32), vm((2 * nz, 2, rows), F32), vm((128, rows), F32),
         vm((2 * rows, 128), F32),
         vm((2, tb, depth), F32),
         vm((ntb, nt - 1, 2, tb, quarter), BF16), vm((ntb, nt - 1, 2, tb, quarter), BF16),
         vm((ntb, 2, tb, quarter), F32),
         vm((half, 2, tb, quarter), BF16), vm((half, 2, tb, quarter), BF16),
         vm((half, nt, 2, tb, quarter), BF16),
-        vm((2, 128, 128), F32), vm((half, 8, 128), F32), vm((half, nt * nz, 8, 128), F32),
+        vm((2, 128, 128), F32), vm((half, 2, 128), F32), vm((half, nt * nz, 2, 128), F32),
         dma((2, 2)), dma((nfb,)), dma((nfb,)),
-        dma, dma((nb,)), dma((nb,)), dma, dma((nb,)),
-        dma, dma((2, nz)), dma((2,)), dma((2, half)),
-        dma, dma((ntb, nt - 1)), dma, dma((half,)),
-        dma, dma((half, nt - 1)), dma, dma((half,)),
+        dma, dma((RING,)), dma((MID_RING,)), dma, dma((RING,)),
+        dma, dma((2,)), dma((2,)), dma((2, half)),
+        dma, dma((ntb,)), dma, dma((half,)),
+        dma, dma((half,)), dma, dma((half,)), dma, dma,
     ]
     return pl.pallas_call(
         functools.partial(line_kernel, (nz, nt, rows, depth, ff, tb, fb)),
@@ -546,7 +667,7 @@
     copies = []
     for k in range(n):
         rows = refs[k].shape[0]
-        cuts = 4 if rows * refs[k].shape[1] > 1 << 20 else 1
+        cuts = CUTS if rows * refs[k].shape[1] > 1 << 20 else 1
         for c in range(cuts):
             span = pl.ds(c * (rows // cuts), rows // cuts)
             copies.append((refs[k].at[span], refs[n + k].at[span]))
@@ -563,7 +684,7 @@
         out_shape=tuple(jax.ShapeDtypeStruct(a.shape, a.dtype) for a in arrays),
         in_specs=[pl.BlockSpec(memory_space=pltpu.VMEM)] * len(arrays),
         out_specs=[pl.BlockSpec(memory_space=pl.ANY)] * len(arrays),
-        scratch_shapes=[pltpu.SemaphoreType.DMA((16,))],
+        scratch_shapes=[pltpu.SemaphoreType.DMA((4 * CUTS,))],
         compiler_params=pltpu.CompilerParams(vmem_limit_bytes=WRITE_LIMIT),
     )(*arrays)
 

time: 129 us -> 123 us (0.953)
  Pallas kernels: 129 us -> 122 us
    pallas_call x1, Pallas kernels: 125 us -> 118 us  [line_call(): pl.pallas_call(functools.partial(line_kernel, (nz, nt, rows, depth, ff, t...]
where the time goes in v3:
time: 123 us
  Pallas kernels  122 us (99%)
    pallas_call x1, Pallas kernels, line_call(): pl.pallas_call(functools.partial(line_kernel, (nz, nt, rows, depth, ff, t...  118 us
    pallas_call x1, Pallas kernels, write_out(): pl.pallas_call(write_kernel, out_shape=tuple((jax.ShapeDtypeStruct(a.shap...  3.76 us

profile of v3, /device:TPU:0, one launch (start us, length us, event | category | flops | bytes accessed | tf_op | source)
XLA Modules:
  0.0 122.9 jit_solution(452704124629814628)
XLA Ops:
  0.6 118.5 %shard_map.75 = (bf16[256,1024]{1,0:T(8,128)(2,1)S(1)}, bf16[256,1024]{1,0:T(8,128)(2,1)S(1)}, bf16[1024,2048]{1,0:T(8,128)(2,1)S(1)}, bf16[2048,1024]{1,0:T(8,128)(2,1)S(1)}) custom-call(bf16[256,1024]{1,0:T(8,128)(2,1)} %tok_in.1, bf16[1024,2048]{1,0:T(8,128)(2,1)} %up_in.1, bf16[2048,1024]{1,0:T(8,128)(2,1)} %down_in.1, bf16[256,1024]{1,0:T(8,128)(2,1)} %cot_in.1), custom_call_target="tpu_custom_call" | custom-call | tf_op jit(solution)/shard_map/pallas_call | solution.py:649
  119.1 3.8 %shard_map.76 = (bf16[256,1024]{1,0:T(8,128)(2,1)}, bf16[256,1024]{1,0:T(8,128)(2,1)}, bf16[1024,2048]{1,0:T(8,128)(2,1)}, bf16[2048,1024]{1,0:T(8,128)(2,1)}) custom-call(bf16[256,1024]{1,0:T(8,128)(2,1)S(1)} %get-tuple-element.8.refs_0_, bf16[256,1024]{1,0:T(8,128)(2,1)S(1)} %get-tuple-element.9.refs_1_, bf16[1024,2048]{1,0:T(8,128)(2,1)S(1)} %get-tuple-element.10.refs_2_, ...), custom_call_target="tpu_custom_call" | custom-call | tf_op jit(solution)/shard_map/pallas_call | solution.py:682

commit v4 on v3

--- a/solution.py
+++ b/solution.py
@@ -48,10 +48,10 @@
     tok_in, up_in, down_in, cot_in,
     mixed, grad, grad_up, grad_down,
     xall, call, nall, cs_tx, cs_rx, wu, wd, tx, rx, rm, hd,
-    st_own, st_tx, st_rx, flip, ms, acc, rs_tx, rs_rx, keep, y_tx, y_rx, ag_rx, square, sq_tx, sq_rx,
+    st_own, st_tx, st_rx, flip, ms, acc, pr_tx, pr_rx, keep, y_tx, y_rx, cr_tx, cr_rx, fin, square, sq_tx, sq_rx, fm_rx,
     load_sem, wu_sem, wd_sem, tx_sem, rx_sem, rm_sem, hs_sem, hr_sem,
-    ss_sem, sr_sem, ys_sem, yr_sem, rss_sem, rsr_sem, yqs_sem, yqr_sem, ags_sem, agr_sem,
-    sqs_sem, sqr_sem, css_sem, csr_sem,
+    ss_sem, sr_sem, ys_sem, yr_sem, prs_sem, prr_sem, yqs_sem, yqr_sem, crs_sem, crr_sem, fis_sem, fir_sem,
+    sqs_sem, sqr_sem, css_sem, csr_sem, fms_sem, fmr_sem,
 ):
     nz, nt, rows, depth, ff, tb_size, fb_size = sizes
     nfb = ff // fb_size
@@ -59,7 +59,7 @@
     half = ntb // 2
     lead = half // 2
     nb = ntb * nfb
-    quarter = depth // nt
+    side = depth // 2
     width = depth * nz
     y = lax.axis_index("fsdp")
     tr = lax.axis_index("trow")
@@ -67,7 +67,10 @@
     mid_low = nz // 2 - 1
     is_mid = jnp.logical_or(j == mid_low, j == mid_low + 1)
     is_end = jnp.logical_not(is_mid)
-    is_odd = lax.rem(tr, 2) == 1
+    core = lax.rem(tr, 2)
+    is_odd = core == 1
+    pair = tr + 1 - 2 * core
+    cross = lax.rem(tr + nt // 2, nt)
     inner = jnp.where(j <= mid_low, j + 1, j - 1)
     outer = jnp.where(j <= mid_low, jnp.maximum(j - 1, 0), jnp.minimum(j + 1, nz - 1))
     lag = jnp.where(is_mid, MID_LAG, END_LAG)
@@ -343,14 +346,50 @@
 
         outward(e).start()
 
-    def rs_copy(t, d, k):
+    def pair_copy(t):
+        return remote(pr_tx.at[t], pr_rx.at[t], prs_sem, prr_sem.at[t], at(y, pair, j))
+
+    def columns(h):
+        return pl.ds(pl.multiple_of(h * side, side), side)
+
+    slot = tr * nz + j
+    everyone = [(a, b) for a in range(nt) for b in range(nz)]
+
+    def mean_copy(t, o, a, b):
         return remote(
-            rs_tx.at[t, d - 1, k], rs_rx.at[t, d - 1, k], rss_sem, rsr_sem.at[t],
-            at(y, t_peer(d), j),
+            sq_tx.at[t], sq_rx.at[o, slot], sqs_sem, sqr_sem.at[o], at(y, t_peer(a), z_peer(b))
         )
 
-    def columns(q):
-        return pl.ds(pl.multiple_of(q * quarter, quarter), quarter)
+    def far_mean(t, o):
+        return remote(sq_tx.at[t], fm_rx.at[o], fms_sem, fmr_sem.at[o], at(other, tr, j))
+
+    def mean_all(o):
+        span = sq_rx.at[o, pl.ds(0, nt * nz - 1)]
+        return remote(span, span, sqs_sem, sqr_sem.at[o], here)
+
+    def spread_means(t, o):
+        far_mean(t, o).wait_recv()
+        sums = sq_tx[t] + fm_rx[o]
+        sq_tx[t] = sums
+        sq_rx[o, slot] = sums
+        for a, b in everyone[1:]:
+            mean_copy(t, o, a, b).start()
+
+    def send_means(t):
+        xhat = xhat_of(t, slice(None))[1]
+        dn = acc[1]
+        square[0, 0:tb_size] = pair_tile(
+            jnp.sum(dn, axis=1, keepdims=True), jnp.sum(dn * xhat, axis=1, keepdims=True)
+        )
+        sq_tx[t] = square[0].T[0:2]
+
+        @pl.when(is_far(t))
+        def _():
+            far_mean(t, t - lead).start()
+
+        @pl.when(t >= lead + half)
+        def _():
+            spread_means(t, t - half)
 
     def use_stage(e):
         f = lax.rem(e, nfb)
@@ -364,18 +403,17 @@
         def _():
             acc[...] = jnp.zeros_like(acc)
 
-        def summed(k):
-            @pl.when(f == nfb - 1)
-            def _():
-                for d in range(1, nt):
-                    rs_tx[t, d - 1, k] = acc[k, :, columns(t_peer(d))].astype(BF16)
-                    rs_copy(t, d, k).start()
-                keep[t, k] = acc[k, :, columns(tr)]
-
         acc[0] += contract(hd[0, f, block_rows(t), :], wd[f], 1, 0)
         acc[1] += contract(hd[1, f, block_rows(t), :], wu[f], 1, 1)
-        summed(0)
-        summed(1)
+
+        @pl.when(f == nfb - 1)
+        def _():
+            for k in range(2):
+                pr_tx[t, k] = acc[k, :, columns(1 - core)].astype(BF16)
+            pair_copy(t).start()
+            for k in range(2):
+                keep[t, k] = acc[k, :, columns(core)]
+            send_means(t)
 
     def first_rows(f, which):
         cols = pl.ds(pl.multiple_of(f * fb_size, fb_size), fb_size)
@@ -396,31 +434,17 @@
     def yq_copy(o):
         return remote(y_tx.at[o], y_rx.at[o], yqs_sem, yqr_sem.at[o], at(other, tr, j))
 
-    def ag_copy(o, d, k):
-        return remote(
-            ag_rx.at[o, tr, k], ag_rx.at[o, tr, k], ags_sem, agr_sem.at[o],
-            at(y, t_peer(d), j),
-        )
-
-    everyone = [(a, b) for a in range(nt) for b in range(nz) if a or b]
-
-    def sq_copy(o, a, b):
-        return remote(
-            sq_tx.at[o], sq_rx.at[o, a * nz + b], sqs_sem, sqr_sem.at[o],
-            at(y, t_peer(a), z_peer(b)),
-        )
-
-    def sq_all(o):
-        span = sq_rx.at[o, pl.ds(1, nt * nz - 1)]
-        return remote(span, span, sqs_sem, sqr_sem.at[o], here)
+    def cross_copy(o, k):
+        return remote(cr_tx.at[o, k], cr_rx.at[o, k], crs_sem, crr_sem.at[o, k], at(y, cross, j))
+
+    def fin_copy(o, k):
+        span = fin.at[o, core, k]
+        return remote(span, span, fis_sem, fir_sem.at[o], at(y, pair, j))
 
     def row_sum_stage(t):
-        remote(rs_tx.at[t], rs_rx.at[t], rss_sem, rsr_sem.at[t], here).wait_recv()
+        pair_copy(t).wait_recv()
         for k in range(2):
-            total = keep[t, k]
-            for d in range(1, nt):
-                total = total + rs_rx[t, d - 1, k].astype(F32)
-            keep[t, k] = total
+            keep[t, k] += pr_rx[t, k].astype(F32)
 
         @pl.when(is_far(t))
         def _():
@@ -430,41 +454,38 @@
 
     def gather_stage(o):
         t = jnp.where(o < lead, o, o + half)
+
+        @pl.when(o < lead)
+        def _():
+            spread_means(t, o)
+
         yq_copy(o).wait_recv()
         for k in range(2):
-            ag_rx[o, tr, k] = (keep[t, k] + y_rx[o, k].astype(F32)).astype(BF16)
-            if k == 0:
-                for d in range(1, nt):
-                    ag_copy(o, d, k).start()
-        dn = ag_rx[o, tr, 1].astype(F32)
-        xhat = xhat_of(t, columns(tr))[1]
-        square[0, 0:tb_size] = pair_tile(
-            jnp.sum(dn, axis=1, keepdims=True), jnp.sum(dn * xhat, axis=1, keepdims=True)
-        )
-        sums = square[0].T[0:2]
-        sq_tx[o] = sums
-        sq_rx[o, 0] = sums
-        for a, b in everyone:
-            sq_copy(o, a, b).start()
-        for d in range(1, nt):
-            ag_copy(o, d, 1).start()
+            cr_tx[o, k] = (keep[t, k] + y_rx[o, k].astype(F32)).astype(BF16)
+            cross_copy(o, k).start()
+
+    def total_stage(o):
+        for k in range(2):
+            cross_copy(o, k).wait_recv()
+            fin[o, core, k] = (cr_tx[o, k].astype(F32) + cr_rx[o, k].astype(F32)).astype(BF16)
+            fin_copy(o, k).start()
 
     def finish_stage(o):
         t = jnp.where(o < lead, o, o + half)
-        span = ag_rx.at[o, pl.ds(0, nt - 1)]
-        remote(span, span, ags_sem, agr_sem.at[o], here).wait_recv()
-        sq_all(o).wait_recv()
+        span = fin.at[o, 0]
+        remote(span, span, fis_sem, fir_sem.at[o], here).wait_recv()
+        mean_all(o).wait_recv()
         total = sq_rx[o, 0]
         for k in range(1, nt * nz):
             total = total + sq_rx[o, k]
         square[1, 0:2] = total / width
         means = square[1].T[0:tb_size]
         rstd = ms[block_rows(t), :][:, 1:2]
-        for q in range(nt):
-            span = slice(q * quarter, (q + 1) * quarter)
+        for h in range(2):
+            span = slice(h * side, (h + 1) * side)
             x, xhat = xhat_of(t, span)
-            mixed[block_rows(o), span] = (x + ag_rx[o, q, 0].astype(F32)).astype(BF16)
-            dn = ag_rx[o, q, 1].astype(F32)
+            mixed[block_rows(o), span] = (x + fin[o, h, 0].astype(F32)).astype(BF16)
+            dn = fin[o, h, 1].astype(F32)
             grad[block_rows(o), span] = (
                 call[block_rows(t), span].astype(F32)
                 + rstd * (dn - means[:, 0:1] - xhat * means[:, 1:2])
@@ -557,33 +578,50 @@
                 with jax.named_scope("gather"):
                     gather_stage(jnp.where(first, t - lead - 1, t - half))
 
+        def total_at(t):
+            @pl.when(jnp.logical_and(t > lead, t <= half))
+            def _():
+                total_stage(t - lead - 1)
+
         done_block(ROW_SHIFT, row_sum_stage)
         done_block(ROW_SHIFT + 1, gather_at)
+        done_block(ROW_SHIFT + 6, total_at)
         return carry
 
     lax.fori_loop(0, nb + max(END_LAG, MID_LAG), step, 0)
 
-    def last_piece(which):
+    def last_piece(which, low, high):
         def body(f, carry):
             last_rows(f, which)
             return carry
 
-        lax.fori_loop(0, nfb, body, 0)
+        lax.fori_loop(low, high, body, 0)
 
     def finish_step(o, carry):
         finish_stage(o)
         return carry
 
-    with jax.named_scope("last_down"):
-        last_piece(0)
+    def total_step(o, carry):
+        total_stage(o)
+        return carry
+
     with jax.named_scope("rowsum"):
         row_sum_stage(ntb - 1)
     with jax.named_scope("gather"):
         gather_stage(half - 1)
-    with jax.named_scope("last_up"):
-        last_piece(1)
+    with jax.named_scope("total"):
+        lax.fori_loop(lead, half - 1, total_step, 0)
     with jax.named_scope("finish"):
-        lax.fori_loop(0, half, finish_step, 0)
+        lax.fori_loop(0, lead, finish_step, 0)
+    with jax.named_scope("last"):
+        last_piece(0, 0, nfb)
+        last_piece(1, 0, nfb // 2)
+    with jax.named_scope("total"):
+        total_stage(half - 1)
+    with jax.named_scope("last"):
+        last_piece(1, nfb // 2, nfb)
+    with jax.named_scope("finish"):
+        lax.fori_loop(lead, half, finish_step, 0)
 
     def sent(ref, sem):
         remote(ref, ref, sem, sem, here).wait_send()
@@ -608,10 +646,12 @@
     def _():
         sent(hd, hs_sem)
 
-    sent(rs_tx, rss_sem)
+    sent(pr_tx, prs_sem)
     sent(y_tx, yqs_sem)
-    sent(ag_rx.at[:, pl.ds(0, nt - 1)], ags_sem)
-    sent(sq_rx.at[:, pl.ds(1, nt * nz - 1)], sqs_sem)
+    sent(cr_tx, crs_sem)
+    sent(fin.at[:, 0], fis_sem)
+    sent(sq_rx.at[:, pl.ds(0, nt * nz - 1)], sqs_sem)
+    sent(fm_rx, fms_sem)
 
 
 def line_call(nz, nt, tokens, w_up, w_down, cotangent):
@@ -622,7 +662,7 @@
     ntb = 2 * rows // tb
     half = ntb // 2
     nb = nfb * ntb
-    quarter = depth // nt
+    side = depth // 2
     sums = -(-nfb // 8) * 8
     vm = pltpu.VMEM
     dma = pltpu.SemaphoreType.DMA
@@ -635,16 +675,15 @@
         vm((rows, 128), F32), vm((2, rows), F32), vm((2 * nz, 2, rows), F32), vm((128, rows), F32),
         vm((2 * rows, 128), F32),
         vm((2, tb, depth), F32),
-        vm((ntb, nt - 1, 2, tb, quarter), BF16), vm((ntb, nt - 1, 2, tb, quarter), BF16),
-        vm((ntb, 2, tb, quarter), F32),
-        vm((half, 2, tb, quarter), BF16), vm((half, 2, tb, quarter), BF16),
-        vm((half, nt, 2, tb, quarter), BF16),
-        vm((2, 128, 128), F32), vm((half, 2, 128), F32), vm((half, nt * nz, 2, 128), F32),
+        vm((ntb, 2, tb, side), BF16), vm((ntb, 2, tb, side), BF16), vm((ntb, 2, tb, side), F32),
+        vm((half, 2, tb, side), BF16), vm((half, 2, tb, side), BF16),
+        vm((half, 2, tb, side), BF16), vm((half, 2, tb, side), BF16), vm((half, 2, 2, tb, side), BF16),
+        vm((2, 128, 128), F32), vm((ntb, 2, 128), F32), vm((half, nt * nz, 2, 128), F32), vm((half, 2, 128), F32),
         dma((2, 2)), dma((nfb,)), dma((nfb,)),
         dma, dma((RING,)), dma((MID_RING,)), dma, dma((RING,)),
         dma, dma((2,)), dma((2,)), dma((2, half)),
         dma, dma((ntb,)), dma, dma((half,)),
-        dma, dma((half,)), dma, dma((half,)), dma, dma,
+        dma, dma((half, 2)), dma, dma((half,)), dma, dma((half,)), dma, dma, dma, dma((half,)),
     ]
     return pl.pallas_call(
         functools.partial(line_kernel, (nz, nt, rows, depth, ff, tb, fb)),
@@ -736,7 +775,7 @@
 
 
 def solution(mesh):
-    fits = mesh.shape["fsdp"] == 2 and mesh.shape["tcol"] == 4
+    fits = mesh.shape["fsdp"] == 2 and mesh.shape["trow"] == 4 and mesh.shape["tcol"] == 4
     return jax.shard_map(
         local_line if fits else local_plain,
         mesh=mesh,

time: 123 us -> 123 us (level)
  no operation moved by 1% of the time
where the time goes in v4:
time: 123 us
  Pallas kernels  122 us (99%)
    pallas_call x1, Pallas kernels, line_call(): pl.pallas_call(functools.partial(line_kernel, (nz, nt, rows, depth, ff, t...  118 us
    pallas_call x1, Pallas kernels, write_out(): pl.pallas_call(write_kernel, out_shape=tuple((jax.ShapeDtypeStruct(a.shap...  3.76 us

profile of v4, /device:TPU:0, one launch (start us, length us, event | category | flops | bytes accessed | tf_op | source)
XLA Modules:
  0.0 122.8 jit_solution(10981110241852474610)
XLA Ops:
  0.6 118.4 %shard_map.75 = (bf16[256,1024]{1,0:T(8,128)(2,1)S(1)}, bf16[256,1024]{1,0:T(8,128)(2,1)S(1)}, bf16[1024,2048]{1,0:T(8,128)(2,1)S(1)}, bf16[2048,1024]{1,0:T(8,128)(2,1)S(1)}) custom-call(bf16[256,1024]{1,0:T(8,128)(2,1)} %tok_in.1, bf16[1024,2048]{1,0:T(8,128)(2,1)} %up_in.1, bf16[2048,1024]{1,0:T(8,128)(2,1)} %down_in.1, bf16[256,1024]{1,0:T(8,128)(2,1)} %cot_in.1), custom_call_target="tpu_custom_call" | custom-call | tf_op jit(solution)/shard_map/pallas_call | solution.py:688
  119.0 3.8 %shard_map.76 = (bf16[256,1024]{1,0:T(8,128)(2,1)}, bf16[256,1024]{1,0:T(8,128)(2,1)}, bf16[1024,2048]{1,0:T(8,128)(2,1)}, bf16[2048,1024]{1,0:T(8,128)(2,1)}) custom-call(bf16[256,1024]{1,0:T(8,128)(2,1)S(1)} %get-tuple-element.8.refs_0_, bf16[256,1024]{1,0:T(8,128)(2,1)S(1)} %get-tuple-element.9.refs_1_, bf16[1024,2048]{1,0:T(8,128)(2,1)S(1)} %get-tuple-element.10.refs_2_, ...), custom_call_target="tpu_custom_call" | custom-call | tf_op jit(solution)/shard_map/pallas_call | solution.py:721

commit v5 on v4

--- a/solution.py
+++ b/solution.py
@@ -15,7 +15,7 @@
 EPS = 1e-05
 END_LAG = 12
 MID_LAG = 3
-ROW_SHIFT = 5
+ROW_SHIFT = 4
 RING = 15
 MID_RING = 10
 COLS_AT = 3
@@ -609,15 +609,13 @@
         row_sum_stage(ntb - 1)
     with jax.named_scope("gather"):
         gather_stage(half - 1)
-    with jax.named_scope("total"):
-        lax.fori_loop(lead, half - 1, total_step, 0)
     with jax.named_scope("finish"):
         lax.fori_loop(0, lead, finish_step, 0)
     with jax.named_scope("last"):
         last_piece(0, 0, nfb)
         last_piece(1, 0, nfb // 2)
     with jax.named_scope("total"):
-        total_stage(half - 1)
+        lax.fori_loop(lead, half, total_step, 0)
     with jax.named_scope("last"):
         last_piece(1, nfb // 2, nfb)
     with jax.named_scope("finish"):

time: 123 us -> 121 us (0.984)
    pallas_call x1, Pallas kernels: 118 us -> 117 us  [line_call(): pl.pallas_call(functools.partial(line_kernel, (nz, nt, rows, depth, ff, t...]
where the time goes in v5:
time: 121 us
  Pallas kernels  121 us (100%)
    pallas_call x1, Pallas kernels, line_call(): pl.pallas_call(functools.partial(line_kernel, (nz, nt, rows, depth, ff, t...  117 us
    pallas_call x1, Pallas kernels, write_out(): pl.pallas_call(write_kernel, out_shape=tuple((jax.ShapeDtypeStruct(a.shap...  3.76 us

profile of v5, /device:TPU:0, one launch (start us, length us, event | category | flops | bytes accessed | tf_op | source)
XLA Modules:
  0.0 121.2 jit_solution(16631222563905101040)
XLA Ops:
  0.6 116.8 %shard_map.75 = (bf16[256,1024]{1,0:T(8,128)(2,1)S(1)}, bf16[256,1024]{1,0:T(8,128)(2,1)S(1)}, bf16[1024,2048]{1,0:T(8,128)(2,1)S(1)}, bf16[2048,1024]{1,0:T(8,128)(2,1)S(1)}) custom-call(bf16[256,1024]{1,0:T(8,128)(2,1)} %tok_in.1, bf16[1024,2048]{1,0:T(8,128)(2,1)} %up_in.1, bf16[2048,1024]{1,0:T(8,128)(2,1)} %down_in.1, bf16[256,1024]{1,0:T(8,128)(2,1)} %cot_in.1), custom_call_target="tpu_custom_call" | custom-call | tf_op jit(solution)/shard_map/pallas_call | solution.py:686
  117.5 3.8 %shard_map.76 = (bf16[256,1024]{1,0:T(8,128)(2,1)}, bf16[256,1024]{1,0:T(8,128)(2,1)}, bf16[1024,2048]{1,0:T(8,128)(2,1)}, bf16[2048,1024]{1,0:T(8,128)(2,1)}) custom-call(bf16[256,1024]{1,0:T(8,128)(2,1)S(1)} %get-tuple-element.8.refs_0_, bf16[256,1024]{1,0:T(8,128)(2,1)S(1)} %get-tuple-element.9.refs_1_, bf16[1024,2048]{1,0:T(8,128)(2,1)S(1)} %get-tuple-element.10.refs_2_, ...), custom_call_target="tpu_custom_call" | custom-call | tf_op jit(solution)/shard_map/pallas_call | solution.py:719
